TPU v7x, 32 devices: a whole 2x2x4 slice. The times are simulated.
32 devices in a mesh: dp: 8 (over z, x), cand: 4 (over y, core).
Axes of the slice: x: 2, y: 2, z: 4, core: 2. Of those that a mesh axis runs over, the one named last changes fastest.
Arguments:
- hidden: bfloat16 [16, 32, 128, 768], P('dp', 'cand'), may hold values from -24 to 24
- attn_weight: bfloat16 [768, 3072], P('dp'), may hold values from -1 to 1
- norm_gain: float32 [768], replicated, may hold values from 0.2 to 4
- pos_bias: float32 [12, 128, 128], replicated, may hold values from -5 to 5
- score_weight: float32 [768], replicated, may hold values from -4 to 4
- pair_lengths: int32 [16, 32], P('dp', 'cand'), may hold values from 32 to 128
- labels: int32 [16, 32], P('dp', 'cand'), may hold values from 0 to 3
Outputs:
- update: float32 [768, 3072], P('dp')
- loss: float32 [16], P('dp')
All inputs are finite; a program needn't handle non-finite values.
Results may differ from a plain program's by a relative error of at most 0.017.
Values may be sent and summed in bfloat16 or wider, within the bound.
A program may use at most 128 MiB of HBM per device.

v0:
```python
import functools

import jax
import jax.numpy as jnp
from jax import lax
from jax.experimental import pallas as pl
from jax.experimental.pallas import tpu as pltpu
from jax.sharding import PartitionSpec as P

EPS = 1e-06
F32 = jnp.float32
BF16 = jnp.bfloat16
VMEM_LIMIT = 60 * 1024 * 1024
NT = (((1,), (1,)), ((), ()))
TN = (((0,), (0,)), ((), ()))


def half_masks(lanes):
    lane = lax.broadcasted_iota(jnp.int32, (1, lanes), 1)
    low = (lane < lanes // 2).astype(F32)
    return low.astype(BF16), (1.0 - low).astype(BF16)


def stack_halves(block, low, high):
    return jnp.concatenate([block * low, block * high], axis=0)


def forward_kernel(hpad, len_ref, h_ref, gain_ref, w_ref, bias_ref, nt_ref, qk_ref, p_ref, u_ref, hsum_ref, norm_scr):
    batch, seq, width = h_ref.shape
    heads = bias_ref.shape[0]
    duo = 2 * (width // heads)
    step = pl.program_id(0)
    values = h_ref[...].reshape(batch * seq, width).astype(F32)
    factor = lax.rsqrt(jnp.mean(values * values, axis=-1, keepdims=True) + EPS)
    normed = (values * factor * gain_ref[...]).astype(BF16)
    norm_scr[...] = normed.reshape(batch, seq, width)
    nt_ref[...] = normed.T
    for part in range(2):
        proj = jnp.dot(normed, w_ref[part], preferred_element_type=F32)
        qk_ref[:, :, part * width : (part + 1) * width] = proj.astype(BF16).reshape(batch, seq, width)
    low, high = half_masks(duo)
    col = lax.broadcasted_iota(jnp.int32, (1, seq), 1)
    row = lax.broadcasted_iota(jnp.int32, (seq, 1), 0)

    def pair(i, carry):
        length = len_ref[step * batch + i]
        penalty = jnp.where(col < length, 0.0, 1.0) > 0.5
        live = row < length
        live2 = jnp.concatenate([live.astype(F32)] * 2, axis=0)
        sums = []
        for hp in range(heads // 2):
            q2 = qk_ref[i, :, hp * duo : (hp + 1) * duo]
            k2 = qk_ref[i, :, width + hp * duo : width + (hp + 1) * duo]
            logits = lax.dot_general(stack_halves(q2, low, high), k2, NT, preferred_element_type=F32)
            logits = logits + bias_ref[2 * hp : 2 * hp + 2].reshape(2 * seq, seq)
            logits = jnp.where(penalty, -1e30, logits)
            expo = jnp.exp(logits - jnp.max(logits, axis=-1, keepdims=True))
            inv = live2 / jnp.sum(expo, axis=-1, keepdims=True)
            probs = (expo * inv).astype(BF16)
            p_ref[i, 2 * hp : 2 * hp + 2] = probs.reshape(2, seq, seq)
            sums.append(jnp.sum(probs.astype(F32).reshape(2, seq, seq), axis=1))
        if hpad > heads:
            sums.append(jnp.zeros((hpad - heads, seq), F32))
        weights = jnp.concatenate(sums, axis=0).astype(BF16)
        u_ref[i] = jnp.dot(weights, norm_scr[i], preferred_element_type=F32).astype(BF16)
        rows = h_ref[i].astype(F32) * live.astype(F32)
        hsum_ref[i] = jnp.sum(rows, axis=0, keepdims=True)
        return carry

    lax.fori_loop(0, batch, pair, 0)


def forward(tokens, pair_len, gain, weights, pos_bias):
    pairs, seq, width = tokens.shape
    heads = pos_bias.shape[0]
    hpad = -(-heads // 16) * 16
    batch = 4 if pairs % 4 == 0 else 1
    full = lambda *shape: pl.BlockSpec(shape, lambda i: (0,) * len(shape))
    return pl.pallas_call(
        functools.partial(forward_kernel, hpad),
        grid=(pairs // batch,),
        in_specs=[
            pl.BlockSpec(memory_space=pltpu.SMEM),
            pl.BlockSpec((batch, seq, width), lambda i: (i, 0, 0)),
            full(1, width),
            full(2, width, width),
            full(heads, seq, seq),
        ],
        out_specs=[
            pl.BlockSpec((width, batch * seq), lambda i: (0, i)),
            pl.BlockSpec((batch, seq, 2 * width), lambda i: (i, 0, 0)),
            pl.BlockSpec((batch, heads, seq, seq), lambda i: (i, 0, 0, 0)),
            pl.BlockSpec((batch, hpad, width), lambda i: (i, 0, 0)),
            pl.BlockSpec((batch, 1, width), lambda i: (i, 0, 0)),
        ],
        out_shape=[
            jax.ShapeDtypeStruct((width, pairs * seq), BF16),
            jax.ShapeDtypeStruct((pairs, seq, 2 * width), BF16),
            jax.ShapeDtypeStruct((pairs, heads, seq, seq), BF16),
            jax.ShapeDtypeStruct((pairs, hpad, width), BF16),
            jax.ShapeDtypeStruct((pairs, 1, width), F32),
        ],
        scratch_shapes=[pltpu.VMEM((batch, seq, width), BF16)],
        compiler_params=pltpu.CompilerParams(vmem_limit_bytes=VMEM_LIMIT),
        cost_estimate=pl.CostEstimate(flops=30_000_000_000, bytes_accessed=24_000_000, transcendentals=0),
        name="attend_forward",
    )(pair_len, tokens, gain, weights, pos_bias)


def head_mask(hpad, width, head_size):
    lane = lax.broadcasted_iota(jnp.int32, (hpad, width), 1)
    head = lax.broadcasted_iota(jnp.int32, (hpad, width), 0)
    start = head * head_size
    return ((lane >= start) & (lane < start + head_size)).astype(F32)


def score_kernel(head_size, u_ref, w_ref, hsum_ref, len_ref, sw_ref, ctx_ref, pooled_ref, score_ref):
    pairs, hpad, width = u_ref.shape
    mixed = jnp.dot(u_ref[...].reshape(pairs * hpad, width), w_ref[0], preferred_element_type=F32)
    mask = head_mask(hpad, width, head_size)
    ctx = jnp.sum(mixed.reshape(pairs, hpad, width) * mask[None], axis=1)
    ctx_ref[...] = ctx.astype(BF16)
    share = 1.0 / len_ref[...]
    mean = ctx * share
    high = mean.astype(BF16)
    low = (mean - high.astype(F32)).astype(BF16)
    both = jnp.dot(jnp.concatenate([high, low], axis=0), w_ref[1], preferred_element_type=F32)
    pooled = hsum_ref[...] * share + both[:pairs] + both[pairs:]
    pooled_ref[...] = pooled
    factor = lax.rsqrt(jnp.mean(pooled * pooled, axis=-1, keepdims=True) + EPS)
    score_ref[...] = jnp.sum(pooled * factor * sw_ref[...], axis=-1, keepdims=True)


def middle_kernel(head_size, sg_ref, pooled_ref, len_ref, sw_ref, u_ref, ctx_ref, w_ref, wc_ref, gvo_ref):
    pairs, hpad, width = u_ref.shape
    pooled = pooled_ref[...]
    sw = sw_ref[...]
    factor = lax.rsqrt(jnp.mean(pooled * pooled, axis=-1, keepdims=True) + EPS)
    dot = jnp.sum(pooled * sw, axis=-1, keepdims=True) * (1.0 / width)
    grad = sg_ref[...] * (factor * sw - pooled * (factor * factor * factor * dot))
    out_grad = (grad / len_ref[...]).astype(BF16)
    cg = lax.dot_general(out_grad, w_ref[1], NT, preferred_element_type=F32).astype(BF16).astype(F32)
    mask = head_mask(hpad, width, head_size)
    spread = (cg[:, None, :] * mask[None]).astype(BF16).reshape(pairs * hpad, width)
    wc = lax.dot_general(spread, w_ref[0], NT, preferred_element_type=F32)
    wc_ref[...] = wc.astype(BF16).reshape(pairs, hpad, width)
    u = u_ref[...].reshape(pairs * hpad, width)
    _, duos, _, lanes = gvo_ref.shape
    gv = lax.dot_general(u, spread, TN, preferred_element_type=F32).astype(BF16)
    go = lax.dot_general(ctx_ref[...], out_grad, TN, preferred_element_type=F32).astype(BF16)
    for j in range(duos):
        gvo_ref[0, j] = gv[:, j * lanes : (j + 1) * lanes]
        gvo_ref[1, j] = go[:, j * lanes : (j + 1) * lanes]


MESH = pl.DeviceIdType.MESH


def greet(targets):
    barrier = pltpu.get_barrier_semaphore()
    for target in targets:
        pl.semaphore_signal(barrier, inc=1, device_id=target, device_id_type=MESH)
    pl.semaphore_wait(barrier, len(targets))


def push(src, dst, send, recv, target):
    copy = pltpu.make_async_remote_copy(
        src_ref=src, dst_ref=dst, send_sem=send, recv_sem=recv, device_id=target, device_id_type=MESH
    )
    copy.start()
    return copy


def gather_kernel(n, m, x_ref, o_ref, own_sem, z_send, x_send, y_send, c_send, recv):
    rows = x_ref.shape[0]
    wide = x_ref.shape[1] // m
    half, duo = n // 2, m // 2
    d, c = lax.axis_index("dp"), lax.axis_index("cand")
    z, x = d // 2, d % 2
    y, core = c // 2, c % 2
    across = (d + 1 - 2 * x, c)
    other = (d, c + 1 - 2 * core)
    zs = [(2 * lax.rem(z + j, half) + x, c) for j in range(1, half)]
    ys = [(d, 2 * lax.rem(y + j, duo) + core) for j in range(1, duo)]
    greet(zs + ys + [across, other])
    mine = x_ref.at[:, pl.ds(pl.multiple_of(c * wide, 128), wide)]
    copies = []
    for j in range(half - 1):
        copies.append(push(mine, o_ref.at[c, d], z_send.at[j], recv.at[c, d], zs[j]))
    copies.append(push(mine, o_ref.at[c, d], x_send.at[0], recv.at[c, d], across))
    local = []
    for k in range(m):
        local.append(
            pltpu.make_async_copy(x_ref.at[:, k * wide : (k + 1) * wide], o_ref.at[k, d], own_sem.at[k])
        )
        local[-1].start()

    def arrived(piece, block):
        ref = o_ref.at[piece, block]
        pltpu.make_async_copy(ref, ref, recv.at[piece, block]).wait()

    def spread(block, slot):
        ref = o_ref.at[c, block]
        for j in range(duo - 1):
            copies.append(push(ref, ref, y_send.at[slot, j], recv.at[c, block], ys[j]))
        copies.append(push(ref, ref, c_send.at[0, slot], recv.at[c, block], other))

    for j in range(1, half):
        block = 2 * lax.rem(z - j + half, half) + x
        arrived(c, block)
        ref = o_ref.at[c, block]
        copies.append(push(ref, ref, x_send.at[j], recv.at[c, block], across))
        spread(block, j - 1)
    far = []
    for j in range(half):
        block = 2 * lax.rem(z - j + half, half) + 1 - x
        arrived(c, block)
        spread(block, half - 1 + j)
    order = [2 * lax.rem(z - j + half, half) + x for j in range(1, half)]
    order += [2 * lax.rem(z - j + half, half) + 1 - x for j in range(half)]
    for slot, block in enumerate(order):
        for j in range(1, duo):
            piece = 2 * lax.rem(y - j + duo, duo) + core
            arrived(piece, block)
            ref = o_ref.at[piece, block]
            copies.append(push(ref, ref, c_send.at[j, slot], recv.at[piece, block], other))
    for slot, block in enumerate(order):
        for j in range(duo):
            arrived(2 * lax.rem(y - j + duo, duo) + 1 - core, block)
    for copy in local:
        copy.wait()
    for copy in copies:
        copy.wait_send()


def gather_weights(block, n, m):
    rows, total = block.shape
    dma = pltpu.SemaphoreType.DMA
    return pl.pallas_call(
        functools.partial(gather_kernel, n, m),
        in_specs=[pl.BlockSpec(memory_space=pltpu.VMEM)],
        out_specs=pl.BlockSpec(memory_space=pltpu.VMEM),
        out_shape=jax.ShapeDtypeStruct((m, n, rows, total // m), block.dtype),
        scratch_shapes=[
            dma((m,)), dma((n // 2,)), dma((n // 2,)), dma((n, max(m // 2 - 1, 1))), dma((m // 2, n)), dma((m, n))
        ],
        compiler_params=pltpu.CompilerParams(
            collective_id=0, has_side_effects=True, vmem_limit_bytes=VMEM_LIMIT
        ),
        name="gather_weights",
    )(block)


def stage_slots(duos, blocks, m):
    plan = []
    x_slot = -1
    for k in range(blocks // m):
        late = (k + 1) * m - 2 * duos
        first = 0 if late <= 0 else 3 * (-(-late // 2) - 1) + 2
        y_slot = first if first == 0 else first + 2
        x_slot = max(y_slot + 1, x_slot) + 3
        for stage, slot in enumerate((first, y_slot, x_slot, x_slot + 3, x_slot + 6)):
            plan.append((slot, stage, k))
    return sorted(plan)


def backward_kernel(n, m, nt_ref, q_ref, k_ref, p_ref, wc_ref, gvo_ref, o_ref, dp_scr, dqk_scr, grads,
                    r1, s1, r2, s2, r3, s3, r4, fin, sq, r6, own,
                    t1, v1, t2, v2, t3, v3, t4, v4, t5, v5, t6, v6):
    pairs, seq, span = q_ref.shape
    duos = dp_scr.shape[0]
    hp = pl.program_id(0)
    chunks, duo, half, _, rows, lanes = r1.shape
    d, c = lax.axis_index("dp"), lax.axis_index("cand")
    z, x = d // 2, d % 2
    y, core = c // 2, c % 2
    across = (d + 1 - 2 * x, c)
    other = (d, c + 1 - 2 * core)

    def arrived(ref, sem):
        pltpu.make_async_copy(ref, ref, sem).wait()

    def stage_core(k):
        push(grads.at[k * duo : (k + 1) * duo, 1 - core], r1.at[k], t1.at[k], v1.at[k], other)

    def stage_y(k):
        arrived(r1.at[k], v1.at[k])
        s1[k] = (grads[k * duo : (k + 1) * duo, core].astype(F32) + r1[k].astype(F32)).astype(BF16)
        for j in range(1, duo):
            peer = lax.rem(y + j, duo)
            push(s1.at[k, peer], r2.at[k, j - 1], t2.at[k, j - 1], v2.at[k, j - 1], (d, 2 * peer + core))

    def stage_x(k):
        total = s1[k, y].astype(F32)
        for j in range(1, duo):
            arrived(r2.at[k, j - 1], v2.at[k, j - 1])
            total = total + r2[k, j - 1].astype(F32)
        s2[k] = total.astype(BF16)
        push(s2.at[k, :, 1 - x], r3.at[k], t3.at[k], v3.at[k], across)

    def stage_z(k):
        arrived(r3.at[k], v3.at[k])
        s3[k] = (s2[k, :, x].astype(F32) + r3[k].astype(F32)).astype(BF16)
        for j in range(1, half):
            peer = lax.rem(z + j, half)
            push(s3.at[k, peer], r4.at[k, j - 1], t4.at[k, j - 1], v4.at[k, j - 1], (2 * peer + x, c))

    def stage_cand(k):
        total = s3[k, z].astype(F32)
        for j in range(1, half):
            arrived(r4.at[k, j - 1], v4.at[k, j - 1])
            total = total + r4[k, j - 1].astype(F32)
        fin[k, c] = total.astype(BF16)
        for j in range(1, m):
            target = (d, lax.rem(c + j, m))
            push(fin.at[k, c], fin.at[k, c], t5.at[k, j - 1], v5.at[k, j - 1], target)

    stages = (stage_core, stage_y, stage_x, stage_z, stage_cand)
    plan = stage_slots(duos, chunks * m, m)

    def run(place):
        for step in range(duos):
            items = [item for item in plan if item[0] == 3 * step + place]
            if items:

                @pl.when(hp == step)
                def _():
                    for _, stage, k in items:
                        stages[stage](k)

    @pl.when(hp == 0)
    def _():
        greet([(d, lax.rem(c + j, m)) for j in range(1, m)] + [(lax.rem(d + j, n), c) for j in range(1, n)])
        load = pltpu.make_async_copy(gvo_ref, grads.at[:duos], own)
        load.start()
        for i in range(pairs):
            part = jnp.dot(wc_ref[i], nt_ref[:, i * seq : (i + 1) * seq], preferred_element_type=F32)
            for j in range(duos):
                dp_scr[j, i] = part[2 * j : 2 * j + 2]
        load.wait()

    run(0)
    low, high = half_masks(span)

    def pair(i, carry):
        probs = p_ref[i].astype(F32)
        term = probs * dp_scr[hp, i][:, None, :]
        dlog = (term - probs * jnp.sum(term, axis=-1, keepdims=True)).astype(BF16)
        wide = jnp.concatenate([dlog[0], dlog[1]], axis=1)
        dq = jnp.dot(wide, stack_halves(k_ref[i], low, high), preferred_element_type=F32)
        dk = lax.dot_general(
            dlog.reshape(2 * seq, seq), stack_halves(q_ref[i], low, high), TN, preferred_element_type=F32
        )
        dqk_scr[i, :, :span] = dq.astype(BF16)
        dqk_scr[i, :, span:] = dk.astype(BF16)
        return carry

    lax.fori_loop(0, pairs, pair, 0, unroll=4)
    run(1)
    grad = jnp.dot(nt_ref[...], dqk_scr[...].reshape(pairs * seq, 2 * span), preferred_element_type=F32)
    grads[duos + hp, 0] = grad[:, :span].reshape(half, 2, rows, lanes).astype(BF16)
    grads[duos + hp, 1] = grad[:, span:].reshape(half, 2, rows, lanes).astype(BF16)
    run(2)

    @pl.when(hp == duos - 1)
    def _():
        for slot, stage, k in plan:
            if slot >= 3 * duos:
                stages[stage](k)
        for k in range(chunks):
            for j in range(1, m):
                arrived(fin.at[k, lax.rem(c - j + m, m)], v5.at[k, j - 1])
        part = jnp.zeros((8, lanes), F32)
        for k in range(chunks):
            block = fin[k].astype(F32).reshape(m * rows // 8, 8, lanes)
            part = part + jnp.sum(block * block, axis=0)
        sq[...] = part
        r6[d] = part
        for j in range(1, n):
            push(sq, r6.at[d], t6.at[j - 1], v6.at[j - 1], (lax.rem(d + j, n), c))
        for j in range(1, n):
            arrived(r6.at[lax.rem(d - j + n, n)], v6.at[j - 1])
        count = chunks * m * lanes * n * rows
        squares = jnp.sum(jnp.sum(jnp.sum(r6[...], axis=0), axis=0, keepdims=True), axis=1, keepdims=True)
        scale = 1.0 / (jnp.sqrt(squares / count) + EPS)
        for k in range(chunks):
            for i in range(m):
                at = k * m + i
                if at < 2 * duos:
                    at = 2 * duos + at
                else:
                    at = (at % 2) * duos + (at - 2 * duos) // 2
                o_ref[:, at * lanes : (at + 1) * lanes] = fin[k, i].astype(F32) * scale
        for k in range(chunks):
            arrived(r1.at[k], t1.at[k])
            arrived(r3.at[k], t3.at[k])
            for j in range(duo - 1):
                arrived(r2.at[k, j], t2.at[k, j])
            for j in range(half - 1):
                arrived(r4.at[k, j], t4.at[k, j])
            for j in range(m - 1):
                arrived(fin.at[k, c], t5.at[k, j])
        for j in range(n - 1):
            arrived(sq, t6.at[j])


def backward(normed_t, qk, probs, wc, gvo, n, m):
    pairs, heads, seq, _ = probs.shape
    width = normed_t.shape[0]
    lanes = 2 * (width // heads)
    duos = heads // 2
    rows, half, duo = width // n, n // 2, m // 2
    chunks = 4 * duos // m
    near, far = max(duo - 1, 1), max(half - 1, 1)
    dma = pltpu.SemaphoreType.DMA
    vmem = pltpu.VMEM
    return pl.pallas_call(
        functools.partial(backward_kernel, n, m),
        grid=(duos,),
        in_specs=[
            pl.BlockSpec((width, pairs * seq), lambda h: (0, 0)),
            pl.BlockSpec((pairs, seq, lanes), lambda h: (0, 0, h)),
            pl.BlockSpec((pairs, seq, lanes), lambda h: (0, 0, duos + h)),
            pl.BlockSpec((pairs, 2, seq, seq), lambda h: (0, h, 0, 0)),
            pl.BlockSpec(wc.shape, lambda h: (0, 0, 0)),
            pl.BlockSpec(memory_space=pl.ANY),
        ],
        out_specs=pl.BlockSpec((rows, 4 * width), lambda h: (0, 0)),
        out_shape=jax.ShapeDtypeStruct((rows, 4 * width), F32),
        scratch_shapes=[
            vmem((duos, pairs, 2, seq), F32),
            vmem((pairs, seq, 2 * lanes), BF16),
            vmem((2 * duos, 2, half, 2, rows, lanes), BF16),
            vmem((chunks, duo, half, 2, rows, lanes), BF16),
            vmem((chunks, duo, half, 2, rows, lanes), BF16),
            vmem((chunks, near, half, 2, rows, lanes), BF16),
            vmem((chunks, half, 2, rows, lanes), BF16),
            vmem((chunks, half, rows, lanes), BF16),
            vmem((chunks, half, rows, lanes), BF16),
            vmem((chunks, far, rows, lanes), BF16),
            vmem((chunks, m, rows, lanes), BF16),
            vmem((8, lanes), F32),
            vmem((n, 8, lanes), F32),
            pltpu.SemaphoreType.DMA,
            dma((chunks,)), dma((chunks,)),
            dma((chunks, near)), dma((chunks, near)),
            dma((chunks,)), dma((chunks,)),
            dma((chunks, far)), dma((chunks, far)),
            dma((chunks, m - 1)), dma((chunks, m - 1)),
            dma((n - 1,)), dma((n - 1,)),
        ],
        compiler_params=pltpu.CompilerParams(
            collective_id=1, has_side_effects=True, vmem_limit_bytes=VMEM_LIMIT
        ),
        cost_estimate=pl.CostEstimate(flops=30_000_000_000, bytes_accessed=20_000_000, transcendentals=0),
        name="backward_reduce",
    )(normed_t, qk, qk, probs, wc, gvo.reshape(duos, 2, half, 2, rows, lanes))


def shards(hidden, attn_weight, norm_gain, pos_bias, score_weight, pair_lengths, labels):
    q_local, c_local, seq, width = hidden.shape
    pairs = q_local * c_local
    heads = pos_bias.shape[0]
    head_size = width // heads
    n, m = lax.axis_size("dp"), lax.axis_size("cand")
    weights = gather_weights(attn_weight, n, m).reshape(4, m // 4, width, 4 * width // m)
    weights = weights.transpose(0, 2, 1, 3).reshape(4, width, width)
    pair_len = pair_lengths.reshape(pairs)
    len_col = pair_len.astype(F32).reshape(pairs, 1)
    gain = norm_gain.reshape(1, width)
    sw = score_weight.reshape(1, width)
    tokens = hidden.reshape(pairs, seq, width)
    normed_t, qk, probs, u, hsum = forward(tokens, pair_len, gain, weights, pos_bias)
    params = pltpu.CompilerParams(vmem_limit_bytes=VMEM_LIMIT)
    whole = lambda *shape: pl.BlockSpec(shape, lambda i: (0,) * len(shape))
    w_spec = pl.BlockSpec((2, width, width), lambda i: (1, 0, 0))
    col, wide = whole(pairs, 1), whole(pairs, width)
    ctx, pooled, score_col = pl.pallas_call(
        functools.partial(score_kernel, head_size),
        grid=(1,),
        in_specs=[whole(*u.shape), w_spec, wide, col, whole(1, width)],
        out_specs=[wide, wide, col],
        out_shape=[
            jax.ShapeDtypeStruct((pairs, width), BF16),
            jax.ShapeDtypeStruct((pairs, width), F32),
            jax.ShapeDtypeStruct((pairs, 1), F32),
        ],
        compiler_params=params,
        name="score_forward",
    )(u, weights, hsum.reshape(pairs, width), len_col, sw)
    scores = score_col.reshape(q_local, c_local)
    mine = jnp.stack([scores, labels.astype(F32)])
    every = lax.all_gather(mine, "cand", axis=2, tiled=True)
    all_scores, all_target = every[0], jnp.exp(every[1])
    highest = jnp.max(all_scores, axis=1)
    expsum = jnp.sum(jnp.exp(all_scores - highest[:, None]), axis=1)
    target_sum = jnp.sum(all_target, axis=1)
    target_dot = jnp.sum(all_target * all_scores, axis=1)
    loss = highest + jnp.log(expsum) - target_dot / target_sum
    target = jnp.exp(labels.astype(F32))
    score_grad = jnp.exp(scores - highest[:, None]) / expsum[:, None] - target / target_sum[:, None]
    duos, duo = heads // 2, 2 * head_size
    wc, gvo = pl.pallas_call(
        functools.partial(middle_kernel, head_size),
        grid=(1,),
        in_specs=[col, wide, col, whole(1, width), whole(*u.shape), wide, w_spec],
        out_specs=[whole(*u.shape), whole(2, duos, width, duo)],
        out_shape=[
            jax.ShapeDtypeStruct(u.shape, BF16),
            jax.ShapeDtypeStruct((2, duos, width, duo), BF16),
        ],
        compiler_params=params,
        name="score_backward",
    )(score_grad.reshape(pairs, 1), pooled, len_col, sw, u, ctx, weights)
    update = backward(normed_t, qk, probs, wc, gvo, n, m)
    return (update, loss)


def solution(mesh):
    in_specs = (
        P("dp", "cand", None, None),
        P("dp", None),
        P(),
        P(),
        P(),
        P("dp", "cand"),
        P("dp", "cand"),
    )
    out_specs = (P("dp", None), P("dp"))
    return jax.shard_map(shards, mesh=mesh, in_specs=in_specs, out_specs=out_specs, check_vma=False)
```

profile of v0, /device:TPU:0, one launch (start us, length us, event | category | flops | bytes accessed | tf_op | source)
XLA Modules:
  0.0 156.0 jit_solution(3299904564447423512)
XLA Ops:
  0.6 1.3 reshape.44.len_ref
  1.9 0.7 convert_element_type.17
  2.6 0.7 convert_bitcast_fusion
  3.3 1.3 reshape.48.sw_ref
  4.5 1.3 reshape.46.gain_ref
  5.8 0.7 convert_element_type.20.len_ref
  6.5 40.8 %gather_weights.1 = bf16[4,8,96,768]{3,2,1,0:T(8,128)(2,1)} custom-call(bf16[96,3072]{1,0:T(8,128)(2,1)} %x_ref.1), custom_call_target="tpu_custom_call" | custom-call | tf_op jit(solution)/shard_map/gather_weights/pallas_call | solution.py:239
  47.3 27.4 %attend_forward.1 = (bf16[768,2048]{1,0:T(8,128)(2,1)}, bf16[16,128,1536]{2,1,0:T(8,128)(2,1)}, bf16[16,12,128,128]{3,2,1,0:T(8,128)(2,1)}, bf16[16,16,768]{2,1,0:T(8,128)(2,1)}, f32[16,1,768]{2,1,0:T(1,128)}) custom-call(s32[16]{0:T(128)} %reshape.44.len_ref, bf16[16,128,768]{2,1,0:T(8,128)(2,1)} %bitcast.23, f32[1,768]{1,0:T(1,128)} %reshape.46.gain_ref, ...), custom_call_target="tpu_custom_call" | custom-call | flops 30000001024 | bytes 24000000 | tf_op jit(solution)/shard_map/attend_forward/pallas_call | solution.py:79
  74.6 1.4 copy.23
  76.1 3.2 %score_forward.1 = (bf16[16,768]{1,0:T(8,128)(2,1)}, f32[16,768]{1,0:T(8,128)}, f32[16,1]{1,0:T(8,128)}) custom-call(bf16[16,16,768]{2,1,0:T(8,128)(2,1)} %get-tuple-element.15.u_ref, bf16[4,768,768]{2,1,0:T(8,128)(2,1)} %bitcast.20, f32[16,768]{1,0:T(8,128)} %bitcast.22, f32[16,1]{1,0:T(8,128)} %convert_element_type.20.len_ref, f32[1,768]{1,0:T(1,128)} %reshape.48.sw_ref), custom_call_target="tpu_custom_call" | custom-call | tf_op jit(solution)/shard_map/score_forward/pallas_call | solution.py:478
  79.3 0.8 reduce.2
  80.1 0.1 stack_reshape.3
  80.2 0.1 reshape.49
  80.3 0.1 copy.16
  80.4 5.2 %all_gather.3 = f32[2,2,32]{1,0,2:T(2,128)S(1)} all-gather(f32[2,2,8]{1,0,2:T(2,128)S(1)} %copy.16), channel_id=1, replica_groups=mesh['dp'=8,'cand'=4] {'cand'}, dimensions={2}, use_global_device_ids=true | all-gather | bytes 640 | tf_op jit(solution)/shard_map/all_gather | solution.py:493
  85.6 0.1 fusion.3
  85.6 0.1 copy.20
  85.7 0.1 copy.17
  85.8 0.2 fusion
  86.0 0.5 divide_subtract_fusion.1
  86.6 0.7 reshape.52.sg_ref
  87.3 5.0 %score_backward.1 = (bf16[16,16,768]{2,1,0:T(8,128)(2,1)}, bf16[2,6,768,128]{3,2,1,0:T(8,128)(2,1)}) custom-call(f32[16,1]{1,0:T(8,128)} %reshape.52.sg_ref, f32[16,768]{1,0:T(8,128)} %get-tuple-element.18.pooled_ref, f32[16,1]{1,0:T(8,128)} %convert_element_type.20.len_ref, f32[1,768]{1,0:T(1,128)} %reshape.48.sw_ref, ...), custom_call_target="tpu_custom_call" | custom-call | tf_op jit(solution)/shard_map/score_backward/pallas_call | solution.py:503
  92.3 61.4 %backward_reduce.1 = f32[96,3072]{1,0:T(8,128)} custom-call(bf16[768,2048]{1,0:T(8,128)(2,1)} %get-tuple-element.12.nt_ref, bf16[16,128,1536]{2,1,0:T(8,128)(2,1)} %get-tuple-element.13.q_ref.k_ref, bf16[16,128,1536]{2,1,0:T(8,128)(2,1)} %get-tuple-element.13.q_ref.k_ref, bf16[16,12,128,128]{3,2,1,0:T(8,128)(2,1)} %get-tuple-element.14.p_ref, ...), custom_call_target="tpu_custom_call" | custom-call | flops 30000001024 | bytes 20000000 | tf_op jit(solution)/shard_map/backward_reduce/pallas_call | solution.py:417
  153.7 2.4 %copy.25 = f32[96,3072]{1,0:T(8,128)} copy(f32[96,3072]{1,0:T(8,128)} %backward_reduce.1) | data formatting | bytes 2359296
  (4 shorter events, 0.1 us)
Async XLA Ops:
  74.6 11.9 %copy-start = (s32[2,8]{1,0:T(2,128)S(1)}, s32[2,8]{1,0:T(2,128)}, u32[]{:S(2)}) copy-start(s32[2,8]{1,0:T(2,128)} %param.13) | copy-start | bytes 196
where the time goes:
time: 157 us; the launch traced here: 156 us
  Pallas kernels  138 us (88%)
  local copies, waits for them, and re-layouts  9.37 us (6%)
  blocking collectives  5.17 us (3%)
  other arithmetic  3.04 us (2%)
    pallas_call x1, Pallas kernels, backward(): pl.pallas_call(functools.partial(backward_kernel, n, m), grid=(duos,), in...  61.4 us
    pallas_call x1, Pallas kernels, gather_weights(): pl.pallas_call(functools.partial(gather_kernel, n, m), in_specs=[pl.Block...  40.8 us
    pallas_call x1, Pallas kernels, forward(): pl.pallas_call(functools.partial(forward_kernel, hpad), grid=(pairs // ba...  27.4 us
    all_gather x1, blocking collectives, shards(): every = lax.all_gather(mine, 'cand', axis=2, tiled=True)  5.17 us
    pallas_call x1, Pallas kernels, shards(): pl.pallas_call(functools.partial(middle_kernel, head_size), grid=(1,), in...  5.03 us
    unnamed x4, local copies, waits for them, and re-layouts  3.79 us
    pallas_call x1, Pallas kernels, shards(): pl.pallas_call(functools.partial(score_kernel, head_size), grid=(1,), in_...  3.25 us

commit v1 on v0

v1 whole, which is shorter than its diff:
```python
import functools

import jax
import jax.numpy as jnp
from jax import lax
from jax.experimental import pallas as pl
from jax.experimental.pallas import tpu as pltpu
from jax.sharding import PartitionSpec as P

EPS = 1e-06
F32 = jnp.float32
BF16 = jnp.bfloat16
VMEM_LIMIT = 60 * 1024 * 1024
NT = (((1,), (1,)), ((), ()))
TN = (((0,), (0,)), ((), ()))
MESH = pl.DeviceIdType.MESH


def half_masks(lanes):
    lane = lax.broadcasted_iota(jnp.int32, (1, lanes), 1)
    low = (lane < lanes // 2).astype(F32)
    return low.astype(BF16), (1.0 - low).astype(BF16)


def stack_halves(block, low, high):
    return jnp.concatenate([block * low, block * high], axis=0)


def head_mask(hpad, width, head_size):
    lane = lax.broadcasted_iota(jnp.int32, (hpad, width), 1)
    head = lax.broadcasted_iota(jnp.int32, (hpad, width), 0)
    start = head * head_size
    return ((lane >= start) & (lane < start + head_size)).astype(F32)


def arrived(ref, sem):
    pltpu.make_async_copy(ref, ref, sem).wait()


def push(src, dst, send, recv, target):
    pltpu.make_async_remote_copy(
        src_ref=src, dst_ref=dst, send_sem=send, recv_sem=recv, device_id=target, device_id_type=MESH
    ).start()


def lengths_column(ref, pairs, per):
    row = lax.broadcasted_iota(jnp.int32, (pairs, 1), 0)
    column = jnp.zeros((pairs, 1), F32)
    for i in range(pairs):
        column = jnp.where(row == i, ref[i // per, i % per].astype(F32), column)
    return column


def fused_kernel(n, m, early, len_ref, lab_ref, h_hbm, w_hbm, gain_ref, bias_hbm, sw_ref,
                 fin, scale_ref, loss_ref,
                 h_scr, bias_scr, w_scr, norm_scr, nt_scr, qk_scr, p_scr, wsum_scr, u_scr, hsum_scr, ex_scr,
                 dp_scr, dqk_scr, grads, r1, s1, r2, s2, r3, s3, r4, sq, r6,
                 h_sem, b_sem, wa_sem, wb_sem,
                 za_s, za_r, xa_s, xa_r, ca_s, zb_s, zb_r, xb_s, xb_r, yb_s, cb_s, g_r, ex_s, ex_r,
                 t1, v1, t2, v2, t3, v3, t4, v4, t5, v5, t6, v6):
    pairs, seq, width = h_scr.shape
    queries, per = len_ref.shape
    heads = bias_scr.shape[0]
    groups, half, _, rows, lanes = w_scr.shape
    duos = heads // 2
    duo = m // 2
    head_size = width // heads
    hpad = u_scr.shape[1]
    batch = pairs // h_sem.shape[0]
    batches = pairs // batch
    early_rounds = early // 2
    late_rounds = (groups - early) // m
    d, c = lax.axis_index("dp"), lax.axis_index("cand")
    z, x = d // 2, d % 2
    y, core = c // 2, c % 2
    across = (d + 1 - 2 * x, c)
    other = (d, c + 1 - 2 * core)

    def column(g):
        late = g // (2 * duos)
        return (1 - late) * (g // 2 + (g % 2) * duos) + late * g

    def early_group(a):
        return 2 * a + core

    def late_group(r):
        return early + r * m + c

    def load(g, sem):
        at = pl.multiple_of(column(g) * lanes, lanes)
        return pltpu.make_async_copy(w_hbm.at[:, pl.ds(at, lanes)], w_scr.at[g, z, x], sem)

    loads = [load(early_group(a), wa_sem.at[a]) for a in range(early_rounds)]
    loads += [load(late_group(r), wb_sem.at[r]) for r in range(late_rounds)]
    tokens = []
    for b in range(batches):
        part = pl.ds(b * batch, batch)
        tokens.append(pltpu.make_async_copy(h_hbm.at[part], h_scr.at[part], h_sem.at[b]))
    bias_load = pltpu.make_async_copy(bias_hbm, bias_scr, b_sem)
    for copy in loads[:1] + tokens[:1] + loads[1:] + tokens[1:] + [bias_load]:
        copy.start()
    peers = [(d, lax.rem(c + j, m)) for j in range(1, m)] + [(lax.rem(d + j, n), c) for j in range(1, n)]
    barrier = pltpu.get_barrier_semaphore()
    for peer in peers:
        pl.semaphore_signal(barrier, inc=1, device_id=peer, device_id_type=MESH)

    col = lax.broadcasted_iota(jnp.int32, (1, seq), 1)
    row = lax.broadcasted_iota(jnp.int32, (seq, 1), 0)
    low, high = half_masks(lanes)
    gain = gain_ref[...].reshape(1, width)
    sw = sw_ref[...].reshape(1, width)

    def length_of(i):
        return len_ref[i // per, i % per]

    def normalise(b):
        tokens[b].wait()
        values = h_scr[b * batch : (b + 1) * batch].reshape(batch * seq, width).astype(F32)
        factor = lax.rsqrt(jnp.mean(values * values, axis=-1, keepdims=True) + EPS)
        normed = (values * factor * gain).astype(BF16)
        norm_scr[b * batch : (b + 1) * batch] = normed.reshape(batch, seq, width)
        nt_scr[:, b * batch * seq : (b + 1) * batch * seq] = normed.T
        for j in range(batch):
            i = b * batch + j
            live = (row < length_of(i)).astype(F32)
            hsum_scr[i : i + 1, :] = jnp.sum(values[j * seq : (j + 1) * seq] * live, axis=0, keepdims=True)

    def send_z(g, s, r):
        for j in range(1, half):
            block = w_scr.at[g, z, x]
            push(block, block, s, r, (2 * lax.rem(z + j, half) + x, c))

    def relay_x(g, z_sem, s, r):
        arrived(w_scr.at[g, 0 : half - 1, 0], z_sem)
        blocks = w_scr.at[g, :, x]
        push(blocks, blocks, s, r, across)

    def early_x(a):
        relay_x(early_group(a), za_r.at[a], xa_s.at[a], xa_r.at[a])

    def early_core(a):
        g = early_group(a)
        arrived(w_scr.at[g, :, 0], xa_r.at[a])
        push(w_scr.at[g], w_scr.at[g], ca_s.at[a], g_r.at[g], other)

    def early_ready(a):
        g = 2 * a + 1 - core
        arrived(w_scr.at[g], g_r.at[g])

    def late_x(r):
        relay_x(late_group(r), zb_r.at[r], xb_s.at[r], xb_r.at[r])

    def late_y(r):
        g = late_group(r)
        arrived(w_scr.at[g, :, 0], xb_r.at[r])
        for j in range(1, duo):
            push(w_scr.at[g], w_scr.at[g], yb_s.at[r, j - 1], g_r.at[g], (d, 2 * lax.rem(y + j, duo) + core))
        push(w_scr.at[g], w_scr.at[g], cb_s.at[r, 0], g_r.at[g], other)

    def late_core(r):
        for j in range(1, duo):
            g = early + r * m + 2 * lax.rem(y - j + duo, duo) + core
            arrived(w_scr.at[g], g_r.at[g])
            push(w_scr.at[g], w_scr.at[g], cb_s.at[r, j], g_r.at[g], other)

    def late_ready(r):
        for j in range(duo):
            g = early + r * m + 2 * j + 1 - core
            arrived(w_scr.at[g], g_r.at[g])

    normalise(0)
    pl.semaphore_wait(barrier, len(peers))
    for a in range(early_rounds):
        loads[a].wait()
        send_z(early_group(a), za_s.at[a], za_r.at[a])
    for r in range(late_rounds):
        loads[early_rounds + r].wait()
        send_z(late_group(r), zb_s.at[r], zb_r.at[r])
    for b in range(1, batches):
        normalise(b)
    early_x(0)
    if early_rounds > 1:
        early_x(1)
    bias_load.wait()
    early_core(0)

    def weight(g):
        value = w_scr[g]
        if rows % 16 == 0:
            return value.reshape(width, lanes)
        return value.astype(F32).reshape(width, lanes).astype(BF16)

    def project(hp, b):
        block = norm_scr[b * batch : (b + 1) * batch].reshape(batch * seq, width)
        both = jnp.concatenate([weight(2 * hp), weight(2 * hp + 1)], axis=1)
        proj = jnp.dot(block, both, preferred_element_type=F32)
        qk_scr[hp, b * batch : (b + 1) * batch] = proj.astype(BF16).reshape(batch, seq, 2 * lanes)

    def attend(hp, i):
        length = length_of(i)
        penalty = jnp.where(col < length, 0.0, 1.0) > 0.5
        live = (row < length).astype(F32)
        live2 = jnp.concatenate([live] * 2, axis=0)
        q2 = qk_scr[hp, i, :, :lanes]
        k2 = qk_scr[hp, i, :, lanes:]
        logits = lax.dot_general(stack_halves(q2, low, high), k2, NT, preferred_element_type=F32)
        logits = logits + bias_scr[pl.ds(2 * hp, 2)].reshape(2 * seq, seq)
        logits = jnp.where(penalty, -1e30, logits)
        expo = jnp.exp(logits - jnp.max(logits, axis=-1, keepdims=True))
        inv = live2 / jnp.sum(expo, axis=-1, keepdims=True)
        probs = (expo * inv).astype(BF16)
        p_scr[hp, i] = probs.reshape(2, seq, seq)
        wsum_scr[hp, i] = jnp.sum(probs.astype(F32).reshape(2, seq, seq), axis=1)

    def forward_step(hp, carry):
        @pl.when(hp + 2 < early_rounds)
        def _():
            early_x(hp + 2)

        @pl.when(hp < early_rounds)
        def _():
            early_ready(hp)

        @pl.when(hp == early_rounds)
        def _():
            late_ready(0)

        for b in range(batches):
            if b == batches // 2:
                @pl.when((hp >= 1) & (hp - 1 < late_rounds))
                def _():
                    late_x(hp - 1)

                @pl.when((hp >= 3) & (hp - 3 < late_rounds))
                def _():
                    late_core(hp - 3)

            if b == batches // 4:
                @pl.when(hp + 1 < early_rounds)
                def _():
                    early_core(hp + 1)

                @pl.when((hp >= 2) & (hp - 2 < late_rounds))
                def _():
                    late_y(hp - 2)

            project(hp, b)
            for j in range(batch):
                attend(hp, b * batch + j)
        return carry

    lax.fori_loop(0, duos, forward_step, 0)
    for r in range(max(duos - 3, 0), late_rounds):
        late_core(r)
    for i in range(pairs):
        parts = [wsum_scr[j, i] for j in range(duos)]
        if hpad > heads:
            parts.append(jnp.zeros((hpad - heads, seq), F32))
        weights = jnp.concatenate(parts, axis=0).astype(BF16)
        u_scr[i] = jnp.dot(weights, norm_scr[i], preferred_element_type=F32).astype(BF16)
    for r in range(1, late_rounds):
        late_ready(r)

    w_v = jnp.concatenate([weight(2 * duos + j) for j in range(duos)], axis=1)
    w_o = jnp.concatenate([weight(3 * duos + j) for j in range(duos)], axis=1)
    u = u_scr[...].reshape(pairs * hpad, width)
    mixed = jnp.dot(u, w_v, preferred_element_type=F32)
    mask = head_mask(hpad, width, head_size)
    ctx32 = jnp.sum(mixed.reshape(pairs, hpad, width) * mask[None], axis=1)
    ctx = ctx32.astype(BF16)
    share = 1.0 / lengths_column(len_ref, pairs, per)
    mean = ctx32 * share
    mean_high = mean.astype(BF16)
    mean_low = (mean - mean_high.astype(F32)).astype(BF16)
    both = jnp.dot(jnp.concatenate([mean_high, mean_low], axis=0), w_o, preferred_element_type=F32)
    pooled = hsum_scr[...] * share + both[:pairs] + both[pairs:]
    factor = lax.rsqrt(jnp.mean(pooled * pooled, axis=-1, keepdims=True) + EPS)
    score = jnp.sum(pooled * factor * sw, axis=-1, keepdims=True)
    label = lengths_column(lab_ref, pairs, per)
    score = jnp.broadcast_to(score, (pairs, lanes))
    label = jnp.broadcast_to(label, (pairs, lanes))
    ex_scr[c] = jnp.concatenate([score, label], axis=0)
    for j in range(1, m):
        push(ex_scr.at[c], ex_scr.at[c], ex_s.at[j - 1], ex_r.at[j - 1], (d, lax.rem(c + j, m)))

    dot = jnp.sum(pooled * sw, axis=-1, keepdims=True) * (1.0 / width)
    slope = (factor * sw - pooled * (factor * factor * factor * dot)) * share
    cg = lax.dot_general(slope.astype(BF16), w_o, NT, preferred_element_type=F32)
    spread = (cg[:, None, :] * mask[None]).astype(BF16).reshape(pairs * hpad, width)
    wc = lax.dot_general(spread, w_v, NT, preferred_element_type=F32)
    u_scr_wc = wc.astype(BF16).reshape(pairs, hpad, width)
    for i in range(pairs):
        part = jnp.dot(u_scr_wc[i], nt_scr[:, i * seq : (i + 1) * seq], preferred_element_type=F32)
        for j in range(duos):
            dp_scr[j, i] = part[2 * j : 2 * j + 2]

    for j in range(1, m):
        arrived(ex_scr.at[lax.rem(c - j + m, m)], ex_r.at[j - 1])
    all_scores, all_labels = ex_scr[:, :pairs], ex_scr[:, pairs:]
    target = jnp.exp(all_labels)
    own_target = jnp.exp(label)
    query = lax.broadcasted_iota(jnp.int32, (pairs, lanes), 0) // per
    loss_row = lax.broadcasted_iota(jnp.int32, loss_ref.shape, 0)
    loss = jnp.zeros(loss_ref.shape, F32)
    score_grad = jnp.zeros((pairs, lanes), F32)

    def total(values):
        return jnp.sum(jnp.sum(values, axis=0), axis=0, keepdims=True)

    for q in range(queries):
        inside = (query == q)[None]
        highest = jnp.max(jnp.max(jnp.where(inside, all_scores, -3e38), axis=0), axis=0, keepdims=True)
        expsum = total(jnp.where(inside, jnp.exp(all_scores - highest[None]), 0.0))
        target_sum = total(jnp.where(inside, target, 0.0))
        target_dot = total(jnp.where(inside, target * all_scores, 0.0))
        loss = jnp.where(loss_row == q, highest + jnp.log(expsum) - target_dot / target_sum, loss)
        own = jnp.exp(score - highest) / expsum - own_target / target_sum
        score_grad = jnp.where(query == q, own, score_grad)
    loss_ref[...] = loss
    sg = score_grad[:, :1]
    out_grad = (slope * sg).astype(BF16)
    spread = (cg * sg).astype(BF16).astype(F32)
    spread = (spread[:, None, :] * mask[None]).astype(BF16).reshape(pairs * hpad, width)
    gv = lax.dot_general(u, spread, TN, preferred_element_type=F32).astype(BF16)
    go = lax.dot_general(ctx, out_grad, TN, preferred_element_type=F32).astype(BF16)
    for t in range(2 * duos):
        source = (gv, go)[t // duos]
        at = (t % duos) * lanes
        grads[t // 2, t % 2] = source[:, at : at + lanes].reshape(half, 2, rows, lanes)
    for i in range(pairs):
        for j in range(duos):
            dp_scr[j, i] = dp_scr[j, i] * sg[i : i + 1]

    chunks = r1.shape[0]

    def stage_core(k):
        push(grads.at[k * duo : (k + 1) * duo, 1 - core], r1.at[k], t1.at[k], v1.at[k], other)

    def stage_y(k):
        arrived(r1.at[k], v1.at[k])
        s1[k] = (grads[k * duo : (k + 1) * duo, core].astype(F32) + r1[k].astype(F32)).astype(BF16)
        for j in range(1, duo):
            peer = lax.rem(y + j, duo)
            push(s1.at[k, peer], r2.at[k, j - 1], t2.at[k, j - 1], v2.at[k, j - 1], (d, 2 * peer + core))

    def stage_x(k):
        value = s1[k, y].astype(F32)
        for j in range(1, duo):
            arrived(r2.at[k, j - 1], v2.at[k, j - 1])
            value = value + r2[k, j - 1].astype(F32)
        s2[k] = value.astype(BF16)
        push(s2.at[k, :, 1 - x], r3.at[k], t3.at[k], v3.at[k], across)

    def stage_z(k):
        arrived(r3.at[k], v3.at[k])
        s3[k] = (s2[k, :, x].astype(F32) + r3[k].astype(F32)).astype(BF16)
        for j in range(1, half):
            peer = lax.rem(z + j, half)
            push(s3.at[k, peer], r4.at[k, j - 1], t4.at[k, j - 1], v4.at[k, j - 1], (2 * peer + x, c))

    def stage_cand(k):
        value = s3[k, z].astype(F32)
        for j in range(1, half):
            arrived(r4.at[k, j - 1], v4.at[k, j - 1])
            value = value + r4[k, j - 1].astype(F32)
        fin[k * m + c] = value.astype(BF16)
        for j in range(1, m):
            piece = fin.at[k * m + c]
            push(piece, piece, t5.at[k, j - 1], v5.at[k, j - 1], (d, lax.rem(c + j, m)))

    stages = (stage_core, stage_y, stage_x, stage_z, stage_cand)
    places = batches + 1
    plan = stage_slots(duos, chunks, m, places)
    last = places * duos

    def run(hp, place):
        for step in range(duos):
            items = [item for item in plan if item[0] == places * step + place]
            if items:
                @pl.when(hp == step)
                def _():
                    for _, stage, k in items:
                        stages[stage](k)

    def backward_step(hp, carry):
        for b in range(batches):
            run(hp, b)
            for j in range(batch):
                i = b * batch + j
                probs = p_scr[hp, i].astype(F32)
                term = probs * dp_scr[hp, i][:, None, :]
                dlog = (term - probs * jnp.sum(term, axis=-1, keepdims=True)).astype(BF16)
                wide = jnp.concatenate([dlog[0], dlog[1]], axis=1)
                q2 = stack_halves(qk_scr[hp, i, :, :lanes], low, high)
                k2 = stack_halves(qk_scr[hp, i, :, lanes:], low, high)
                dq = jnp.dot(wide, k2, preferred_element_type=F32)
                dk = lax.dot_general(dlog.reshape(2 * seq, seq), q2, TN, preferred_element_type=F32)
                dqk_scr[i, :, :lanes] = dq.astype(BF16)
                dqk_scr[i, :, lanes:] = dk.astype(BF16)
        grad = jnp.dot(nt_scr[...], dqk_scr[...].reshape(pairs * seq, 2 * lanes), preferred_element_type=F32)
        grads[duos + hp, 0] = grad[:, :lanes].reshape(half, 2, rows, lanes).astype(BF16)
        grads[duos + hp, 1] = grad[:, lanes:].reshape(half, 2, rows, lanes).astype(BF16)
        run(hp, batches)
        return carry

    lax.fori_loop(0, duos, backward_step, 0)
    for slot, stage, k in plan:
        if slot >= last:
            stages[stage](k)
    for k in range(chunks):
        for j in range(1, m):
            arrived(fin.at[k * m + lax.rem(c - j + m, m)], v5.at[k, j - 1])
    part = jnp.zeros((8, lanes), F32)
    for g in range(groups):
        block = fin[g].astype(F32).reshape(rows // 8, 8, lanes)
        part = part + jnp.sum(block * block, axis=0)
    sq[...] = part
    r6[d] = part
    for j in range(1, n):
        push(sq, r6.at[d], t6.at[j - 1], v6.at[j - 1], (lax.rem(d + j, n), c))
    for j in range(1, n):
        arrived(r6.at[lax.rem(d - j + n, n)], v6.at[j - 1])
    count = groups * lanes * n * rows
    squares = jnp.sum(jnp.sum(jnp.sum(r6[...], axis=0), axis=0, keepdims=True), axis=1, keepdims=True)
    scale_ref[...] = jnp.broadcast_to(1.0 / (jnp.sqrt(squares / count) + EPS), scale_ref.shape)

    for a in range(early_rounds):
        arrived(w_scr.at[0, 0 : half - 1, 0], za_s.at[a])
        arrived(w_scr.at[0, :, 0], xa_s.at[a])
        arrived(w_scr.at[0], ca_s.at[a])
    for r in range(late_rounds):
        arrived(w_scr.at[0, 0 : half - 1, 0], zb_s.at[r])
        arrived(w_scr.at[0, :, 0], xb_s.at[r])
        for j in range(duo - 1):
            arrived(w_scr.at[0], yb_s.at[r, j])
        for j in range(duo):
            arrived(w_scr.at[0], cb_s.at[r, j])
    for j in range(m - 1):
        arrived(ex_scr.at[c], ex_s.at[j])
    for k in range(chunks):
        arrived(r1.at[k], t1.at[k])
        arrived(r3.at[k], t3.at[k])
        for j in range(duo - 1):
            arrived(r2.at[k, j], t2.at[k, j])
        for j in range(half - 1):
            arrived(r4.at[k, j], t4.at[k, j])
        for j in range(m - 1):
            arrived(fin.at[k * m + c], t5.at[k, j])
    for j in range(n - 1):
        arrived(sq, t6.at[j])


def stage_slots(duos, chunks, m, places):
    plan = []
    previous = [0] * 5
    for k in range(chunks):
        done = (k + 1) * m - 2 * duos
        first = 0 if done <= 0 else places * (-(-done // 2)) - 1
        slots = [first]
        for gap in (2, 6, 4, 4):
            slots.append(slots[-1] + gap)
        for stage in range(5):
            slots[stage] = max(slots[stage], previous[stage] + (0 if stage == 0 else 3))
            if stage:
                slots[stage] = max(slots[stage], slots[stage - 1] + 1)
            plan.append((slots[stage], stage, k))
        previous = slots
    return sorted(plan)


def finish_kernel(duos, fin, scale_ref, loss_in, out_ref, loss_ref):
    groups, rows, lanes = fin.shape
    scale = scale_ref[0:1, :]
    for at in range(groups):
        if at < 2 * duos:
            col = 2 * duos + at
        else:
            col = (at % 2) * duos + (at - 2 * duos) // 2
        out_ref[:, col * lanes : (col + 1) * lanes] = fin[at].astype(F32) * scale
    for q in range(loss_ref.shape[0]):
        loss_ref[q] = jnp.max(loss_in[q : q + 1, :])


def shards(hidden, attn_weight, norm_gain, pos_bias, score_weight, pair_lengths, labels):
    queries, per, seq, width = hidden.shape
    pairs = queries * per
    heads = pos_bias.shape[0]
    n, m = lax.axis_size("dp"), lax.axis_size("cand")
    lanes = 2 * (width // heads)
    duos = heads // 2
    groups = 4 * duos
    rows, half, duo = width // n, n // 2, m // 2
    early = groups // 3
    early_rounds, late_rounds = early // 2, (groups - early) // m
    batch = 4 if pairs % 4 == 0 else 1
    hpad = -(-heads // 16) * 16
    chunks = groups // m
    near, far = max(duo - 1, 1), max(half - 1, 1)
    dma = pltpu.SemaphoreType.DMA
    vmem = pltpu.VMEM
    here = pl.BlockSpec(memory_space=pltpu.VMEM)
    away = pl.BlockSpec(memory_space=pl.ANY)
    small = pl.BlockSpec(memory_space=pltpu.SMEM)
    loss_rows = -(-queries // 8) * 8
    fin, scale, loss = pl.pallas_call(
        functools.partial(fused_kernel, n, m, early),
        in_specs=[small, small, away, away, here, away, here],
        out_specs=[here, here, here],
        out_shape=[
            jax.ShapeDtypeStruct((groups, rows, lanes), BF16),
            jax.ShapeDtypeStruct((8, lanes), F32),
            jax.ShapeDtypeStruct((loss_rows, lanes), F32),
        ],
        scratch_shapes=[
            vmem((pairs, seq, width), BF16),
            vmem(pos_bias.shape, F32),
            vmem((groups, half, 2, rows, lanes), BF16),
            vmem((pairs, seq, width), BF16),
            vmem((width, pairs * seq), BF16),
            vmem((duos, pairs, seq, 2 * lanes), BF16),
            vmem((duos, pairs, 2, seq, seq), BF16),
            vmem((duos, pairs, 2, seq), F32),
            vmem((pairs, hpad, width), BF16),
            vmem((pairs, width), F32),
            vmem((m, 2 * pairs, lanes), F32),
            vmem((duos, pairs, 2, seq), F32),
            vmem((pairs, seq, 2 * lanes), BF16),
            vmem((2 * duos, 2, half, 2, rows, lanes), BF16),
            vmem((chunks, duo, half, 2, rows, lanes), BF16),
            vmem((chunks, duo, half, 2, rows, lanes), BF16),
            vmem((chunks, near, half, 2, rows, lanes), BF16),
            vmem((chunks, half, 2, rows, lanes), BF16),
            vmem((chunks, half, rows, lanes), BF16),
            vmem((chunks, half, rows, lanes), BF16),
            vmem((chunks, far, rows, lanes), BF16),
            vmem((8, lanes), F32),
            vmem((n, 8, lanes), F32),
            dma((pairs // batch,)), dma, dma((early_rounds,)), dma((late_rounds,)),
            dma((early_rounds,)), dma((early_rounds,)), dma((early_rounds,)), dma((early_rounds,)),
            dma((early_rounds,)),
            dma((late_rounds,)), dma((late_rounds,)), dma((late_rounds,)), dma((late_rounds,)),
            dma((late_rounds, near)), dma((late_rounds, duo)), dma((groups,)),
            dma((m - 1,)), dma((m - 1,)),
            dma((chunks,)), dma((chunks,)),
            dma((chunks, near)), dma((chunks, near)),
            dma((chunks,)), dma((chunks,)),
            dma((chunks, far)), dma((chunks, far)),
            dma((chunks, m - 1)), dma((chunks, m - 1)),
            dma((n - 1,)), dma((n - 1,)),
        ],
        compiler_params=pltpu.CompilerParams(
            collective_id=0, has_side_effects=True, vmem_limit_bytes=VMEM_LIMIT
        ),
        name="fused_step",
    )(pair_lengths, labels, hidden.reshape(pairs, seq, width), attn_weight, norm_gain, pos_bias, score_weight)
    update, loss = pl.pallas_call(
        functools.partial(finish_kernel, duos),
        in_specs=[here, here, here],
        out_specs=[here, small],
        out_shape=[
            jax.ShapeDtypeStruct((rows, 4 * width), F32),
            jax.ShapeDtypeStruct((queries,), F32),
        ],
        name="finish",
    )(fin, scale, loss)
    return (update, loss)


def solution(mesh):
    in_specs = (
        P("dp", "cand", None, None),
        P("dp", None),
        P(),
        P(),
        P(),
        P("dp", "cand"),
        P("dp", "cand"),
    )
    out_specs = (P("dp", None), P("dp"))
    return jax.shard_map(shards, mesh=mesh, in_specs=in_specs, out_specs=out_specs, check_vma=False)
```

time: 157 us -> 125 us (0.80)
  Pallas kernels: 138 us -> 124 us
  local copies, waits for them, and re-layouts: 9.37 us -> 0 us
  blocking collectives: 5.17 us -> 0 us
  other arithmetic: 3.04 us -> 0 us
    pallas_call x5 -> x2, Pallas kernels: 138 us -> 124 us  [the longest x1 121 us: shards(): pl.pallas_call(functools.partial(fused_kernel, n, m, early), in_specs=[sm...]
    all_gather x1 -> x0, blocking collectives: 5.17 us -> none  [shards(): every = lax.all_gather(mine, 'cand', axis=2, tiled=True)]
    reshape x5 -> x0, local copies, waits for them, and re-layouts: 4.59 us -> none  [the longest x1 1.28 us: shards(): gain = norm_gain.reshape(1, width)]
    unnamed x4 -> x0, local copies, waits for them, and re-layouts: 3.79 us -> none
where the time goes in v1:
time: 125 us; the launch traced here: 124 us
  Pallas kernels  124 us (99%)
    pallas_call x1, Pallas kernels, shards(): pl.pallas_call(functools.partial(fused_kernel, n, m, early), in_specs=[sm...  121 us

profile of v1, /device:TPU:0, one launch (start us, length us, event | category | flops | bytes accessed | tf_op | source)
XLA Modules:
  0.0 124.4 jit_solution(4302620764876247540)
XLA Ops:
  0.6 121.4 %fused_step.1 = (bf16[24,96,128]{2,1,0:T(8,128)(2,1)}, f32[8,128]{1,0:T(8,128)}, f32[8,128]{1,0:T(8,128)}) custom-call(s32[2,8]{1,0:T(2,128)} %len_ref.1, s32[2,8]{1,0:T(2,128)} %lab_ref.1, bf16[16,128,768]{2,1,0:T(8,128)(2,1)} %bitcast.1, bf16[96,3072]{1,0:T(8,128)(2,1)} %w_hbm.1, f32[768]{0:T(1024)} %gain_ref.1, f32[12,128,128]{2,1,0:T(8,128)} %bias_hbm.1, ...), custom_call_target="tpu_custom_call" | custom-call | tf_op jit(solution)/shard_map/fused_step/pallas_call | solution.py:505
  122.0 2.2 %finish.1 = (f32[96,3072]{1,0:T(8,128)}, f32[2]{0:T(128)}) custom-call(bf16[24,96,128]{2,1,0:T(8,128)(2,1)} %get-tuple-element.5.fin, f32[8,128]{1,0:T(8,128)} %get-tuple-element.6.scale_ref, f32[8,128]{1,0:T(8,128)} %get-tuple-element.7.loss_in), custom_call_target="tpu_custom_call" | custom-call | tf_op jit(solution)/shard_map/finish/pallas_call | solution.py:556

commit v2 on v1

--- a/solution.py
+++ b/solution.py
@@ -54,10 +54,11 @@
 def fused_kernel(n, m, early, len_ref, lab_ref, h_hbm, w_hbm, gain_ref, bias_hbm, sw_ref,
                  fin, scale_ref, loss_ref,
                  h_scr, bias_scr, w_scr, norm_scr, nt_scr, qk_scr, p_scr, wsum_scr, u_scr, hsum_scr, ex_scr,
-                 dp_scr, dqk_scr, grads, r1, s1, r2, s2, r3, s3, r4, sq, r6,
+                 dp_scr, dqk_scr, grads, r1, s1, r2, s2, r3, s3, r4, a1, b1, a2, b2, a3, a4, sq, r6,
                  h_sem, b_sem, wa_sem, wb_sem,
-                 za_s, za_r, xa_s, xa_r, ca_s, zb_s, zb_r, xb_s, xb_r, yb_s, cb_s, g_r, ex_s, ex_r,
-                 t1, v1, t2, v2, t3, v3, t4, v4, t5, v5, t6, v6):
+                 za_s, za_r, xa_s, xa_r, ca_s, zb_s, zb_r, xb_s, xb_r, yb_s, yb_r, cb_s, g_r, ex_s, ex_r,
+                 t1, v1, t2, v2, t3, v3, t4, v4, t5, v5, t6, v6,
+                 e1, f1, e2, f2, e3, f3, e4, f4, e5, f5):
     pairs, seq, width = h_scr.shape
     queries, per = len_ref.shape
     heads = bias_scr.shape[0]
@@ -76,22 +77,27 @@
     across = (d + 1 - 2 * x, c)
     other = (d, c + 1 - 2 * core)
 
+    split = early_rounds // 2
+    late = duos - early_rounds
+
     def column(g):
-        late = g // (2 * duos)
-        return (1 - late) * (g // 2 + (g % 2) * duos) + late * g
-
-    def early_group(a):
-        return 2 * a + core
-
-    def late_group(r):
-        return early + r * m + c
+        tail = g // (2 * duos)
+        return (1 - tail) * (g // 2 + (g % 2) * duos) + tail * g
+
+    def early_group(a, which):
+        return 2 * (a + late * (a // split)) + which
+
+    def late_group(r, which):
+        if r == 0:
+            return 2 * split + which + (early - 2 * split) * (which // (2 * late))
+        return early + r * m + which
 
     def load(g, sem):
         at = pl.multiple_of(column(g) * lanes, lanes)
         return pltpu.make_async_copy(w_hbm.at[:, pl.ds(at, lanes)], w_scr.at[g, z, x], sem)
 
-    loads = [load(early_group(a), wa_sem.at[a]) for a in range(early_rounds)]
-    loads += [load(late_group(r), wb_sem.at[r]) for r in range(late_rounds)]
+    loads = [load(early_group(a, core), wa_sem.at[a]) for a in range(early_rounds)]
+    loads += [load(late_group(r, c), wb_sem.at[r]) for r in range(late_rounds)]
     tokens = []
     for b in range(batches):
         part = pl.ds(b * batch, batch)
@@ -106,6 +112,8 @@
 
     col = lax.broadcasted_iota(jnp.int32, (1, seq), 1)
     row = lax.broadcasted_iota(jnp.int32, (seq, 1), 0)
+    key = lax.broadcasted_iota(jnp.int32, (2, seq, seq), 1)
+    ones = jnp.ones((16, seq), BF16)
     low, high = half_masks(lanes)
     gain = gain_ref[...].reshape(1, width)
     sw = sw_ref[...].reshape(1, width)
@@ -136,53 +144,70 @@
         push(blocks, blocks, s, r, across)
 
     def early_x(a):
-        relay_x(early_group(a), za_r.at[a], xa_s.at[a], xa_r.at[a])
+        relay_x(early_group(a, core), za_r.at[a], xa_s.at[a], xa_r.at[a])
 
     def early_core(a):
-        g = early_group(a)
+        g = early_group(a, core)
         arrived(w_scr.at[g, :, 0], xa_r.at[a])
         push(w_scr.at[g], w_scr.at[g], ca_s.at[a], g_r.at[g], other)
 
     def early_ready(a):
-        g = 2 * a + 1 - core
+        g = early_group(a, 1 - core)
         arrived(w_scr.at[g], g_r.at[g])
 
+    def relay_y(r, side, place):
+        blocks = w_scr.at[late_group(r, c), :, side]
+        for j in range(1, duo):
+            target = (d, 2 * lax.rem(y + j, duo) + core)
+            push(blocks, blocks, yb_s.at[r, place, j - 1], yb_r.at[r, place, j - 1], target)
+
     def late_x(r):
-        relay_x(late_group(r), zb_r.at[r], xb_s.at[r], xb_r.at[r])
+        relay_x(late_group(r, c), zb_r.at[r], xb_s.at[r], xb_r.at[r])
+        relay_y(r, x, 0)
 
     def late_y(r):
-        g = late_group(r)
+        g = late_group(r, c)
         arrived(w_scr.at[g, :, 0], xb_r.at[r])
-        for j in range(1, duo):
-            push(w_scr.at[g], w_scr.at[g], yb_s.at[r, j - 1], g_r.at[g], (d, 2 * lax.rem(y + j, duo) + core))
+        relay_y(r, 1 - x, 1)
         push(w_scr.at[g], w_scr.at[g], cb_s.at[r, 0], g_r.at[g], other)
 
     def late_core(r):
         for j in range(1, duo):
-            g = early + r * m + 2 * lax.rem(y - j + duo, duo) + core
-            arrived(w_scr.at[g], g_r.at[g])
+            g = late_group(r, 2 * lax.rem(y - j + duo, duo) + core)
+            for place in range(2):
+                arrived(w_scr.at[g, :, 0], yb_r.at[r, place, j - 1])
             push(w_scr.at[g], w_scr.at[g], cb_s.at[r, j], g_r.at[g], other)
 
     def late_ready(r):
         for j in range(duo):
-            g = early + r * m + 2 * j + 1 - core
+            g = late_group(r, 2 * j + 1 - core)
             arrived(w_scr.at[g], g_r.at[g])
 
-    normalise(0)
-    pl.semaphore_wait(barrier, len(peers))
-    for a in range(early_rounds):
-        loads[a].wait()
-        send_z(early_group(a), za_s.at[a], za_r.at[a])
-    for r in range(late_rounds):
-        loads[early_rounds + r].wait()
-        send_z(late_group(r), zb_s.at[r], zb_r.at[r])
-    for b in range(1, batches):
-        normalise(b)
-    early_x(0)
-    if early_rounds > 1:
-        early_x(1)
-    bias_load.wait()
-    early_core(0)
+    def relays(todo):
+        for act, r in todo:
+            if r < (early_rounds if act in (early_x, early_core, early_ready) else late_rounds):
+                act(r)
+
+    with jax.named_scope('norm0'):
+        normalise(0)
+    with jax.named_scope('barrier'):
+        pl.semaphore_wait(barrier, len(peers))
+    for r in range(max(early_rounds, late_rounds)):
+        if r < early_rounds:
+            loads[r].wait()
+            send_z(early_group(r, core), za_s.at[r], za_r.at[r])
+        if r < late_rounds:
+            loads[early_rounds + r].wait()
+            send_z(late_group(r, c), zb_s.at[r], zb_r.at[r])
+    with jax.named_scope('norm'):
+        for b in range(1, batches):
+            normalise(b)
+    with jax.named_scope('bias'):
+        bias_load.wait()
+        for h in range(heads):
+            bias_scr[h] = bias_scr[h].T
+    with jax.named_scope('early'):
+        relays([(early_x, 0), (late_x, 0), (early_core, 0), (early_x, 1)])
 
     def weight(g):
         value = w_scr[g]
@@ -190,75 +215,76 @@
             return value.reshape(width, lanes)
         return value.astype(F32).reshape(width, lanes).astype(BF16)
 
-    def project(hp, b):
-        block = norm_scr[b * batch : (b + 1) * batch].reshape(batch * seq, width)
+    def project(hp):
         both = jnp.concatenate([weight(2 * hp), weight(2 * hp + 1)], axis=1)
-        proj = jnp.dot(block, both, preferred_element_type=F32)
-        qk_scr[hp, b * batch : (b + 1) * batch] = proj.astype(BF16).reshape(batch, seq, 2 * lanes)
+        for b in range(batches):
+            block = norm_scr[b * batch : (b + 1) * batch].reshape(batch * seq, width)
+            proj = jnp.dot(block, both, preferred_element_type=F32)
+            qk_scr[hp, b * batch : (b + 1) * batch] = proj.astype(BF16).reshape(batch, seq, 2 * lanes)
 
     def attend(hp, i):
         length = length_of(i)
-        penalty = jnp.where(col < length, 0.0, 1.0) > 0.5
-        live = (row < length).astype(F32)
-        live2 = jnp.concatenate([live] * 2, axis=0)
+        live = (col < length).astype(F32)
         q2 = qk_scr[hp, i, :, :lanes]
         k2 = qk_scr[hp, i, :, lanes:]
-        logits = lax.dot_general(stack_halves(q2, low, high), k2, NT, preferred_element_type=F32)
-        logits = logits + bias_scr[pl.ds(2 * hp, 2)].reshape(2 * seq, seq)
-        logits = jnp.where(penalty, -1e30, logits)
-        expo = jnp.exp(logits - jnp.max(logits, axis=-1, keepdims=True))
-        inv = live2 / jnp.sum(expo, axis=-1, keepdims=True)
+        logits = lax.dot_general(stack_halves(k2, low, high), q2, NT, preferred_element_type=F32)
+        logits = logits.reshape(2, seq, seq) + bias_scr[pl.ds(2 * hp, 2)]
+        logits = jnp.where(key < length, logits, -1e30)
+        expo = jnp.exp(logits - jnp.max(logits, axis=1, keepdims=True))
+        inv = live[None] / jnp.sum(expo, axis=1, keepdims=True)
         probs = (expo * inv).astype(BF16)
-        p_scr[hp, i] = probs.reshape(2, seq, seq)
-        wsum_scr[hp, i] = jnp.sum(probs.astype(F32).reshape(2, seq, seq), axis=1)
+        p_scr[hp, i] = probs
+        sums = lax.dot_general(ones, probs.reshape(2 * seq, seq), NT, preferred_element_type=F32)
+        wsum_scr[hp, i, 0:1] = sums[:1, :seq]
+        wsum_scr[hp, i, 1:2] = sums[:1, seq:]
+
+    forward_plan = {
+        (0, 0): [(early_ready, 0)],
+        (0, 1): [(late_y, 0), (late_x, 1)],
+        (1, 0): [(early_core, 1), (early_x, 2), (early_ready, 1)],
+        (1, 1): [(late_x, 2)],
+        (2, 0): [(late_y, 1), (late_core, 0), (late_ready, 0)],
+        (2, 1): [(early_core, 2), (early_x, 3)],
+        (3, 0): [(late_y, 2), (late_x, 3)],
+        (3, 1): [(late_core, 1)],
+        (4, 0): [(early_ready, 2), (early_core, 3)],
+        (4, 1): [(late_y, 3)],
+        (5, 0): [(early_ready, 3), (late_core, 2)],
+    }
 
     def forward_step(hp, carry):
-        @pl.when(hp + 2 < early_rounds)
-        def _():
-            early_x(hp + 2)
-
-        @pl.when(hp < early_rounds)
-        def _():
-            early_ready(hp)
-
-        @pl.when(hp == early_rounds)
-        def _():
-            late_ready(0)
-
-        for b in range(batches):
-            if b == batches // 2:
-                @pl.when((hp >= 1) & (hp - 1 < late_rounds))
-                def _():
-                    late_x(hp - 1)
-
-                @pl.when((hp >= 3) & (hp - 3 < late_rounds))
-                def _():
-                    late_core(hp - 3)
-
-            if b == batches // 4:
-                @pl.when(hp + 1 < early_rounds)
-                def _():
-                    early_core(hp + 1)
-
-                @pl.when((hp >= 2) & (hp - 2 < late_rounds))
-                def _():
-                    late_y(hp - 2)
-
-            project(hp, b)
-            for j in range(batch):
-                attend(hp, b * batch + j)
+        for place in range(2):
+            with jax.named_scope('fw_relay'):
+                for step in range(duos):
+                    todo = forward_plan.get((step, place))
+                    if todo:
+                        @pl.when(hp == step)
+                        def _():
+                            relays(todo)
+
+            @pl.when(hp < duos)
+            def _():
+                with jax.named_scope('fw_block'):
+                    if place == 0:
+                        project(hp)
+                    else:
+                        for i in range(pairs):
+                            attend(hp, i)
+
         return carry
 
     lax.fori_loop(0, duos, forward_step, 0)
-    for r in range(max(duos - 3, 0), late_rounds):
-        late_core(r)
-    for i in range(pairs):
+    with jax.named_scope('late_core'):
+        relays([(late_core, 3)])
+    with jax.named_scope('u'):
+      for i in range(pairs):
         parts = [wsum_scr[j, i] for j in range(duos)]
         if hpad > heads:
             parts.append(jnp.zeros((hpad - heads, seq), F32))
         weights = jnp.concatenate(parts, axis=0).astype(BF16)
         u_scr[i] = jnp.dot(weights, norm_scr[i], preferred_element_type=F32).astype(BF16)
-    for r in range(1, late_rounds):
+    with jax.named_scope('late_ready'):
+      for r in range(1, late_rounds):
         late_ready(r)
 
     w_v = jnp.concatenate([weight(2 * duos + j) for j in range(duos)], axis=1)
@@ -294,7 +320,8 @@
         for j in range(duos):
             dp_scr[j, i] = part[2 * j : 2 * j + 2]
 
-    for j in range(1, m):
+    with jax.named_scope('ex_wait'):
+      for j in range(1, m):
         arrived(ex_scr.at[lax.rem(c - j + m, m)], ex_r.at[j - 1])
     all_scores, all_labels = ex_scr[:, :pairs], ex_scr[:, pairs:]
     target = jnp.exp(all_labels)
@@ -368,48 +395,116 @@
             piece = fin.at[k * m + c]
             push(piece, piece, t5.at[k, j - 1], v5.at[k, j - 1], (d, lax.rem(c + j, m)))
 
+    def pair_core(k):
+        push(grads.at[chunks * duo + k, 1 - core], a1.at[k], e1.at[k], f1.at[k], other)
+
+    def pair_x(k):
+        arrived(a1.at[k], f1.at[k])
+        b1[k] = (grads[chunks * duo + k, core].astype(F32) + a1[k].astype(F32)).astype(BF16)
+        push(b1.at[k, :, 1 - x], a2.at[k], e2.at[k], f2.at[k], across)
+
+    def pair_z(k):
+        arrived(a2.at[k], f2.at[k])
+        b2[k] = (b1[k, :, x].astype(F32) + a2[k].astype(F32)).astype(BF16)
+        for j in range(1, half):
+            peer = lax.rem(z + j, half)
+            push(b2.at[k, peer], a3.at[k, j - 1], e3.at[k, j - 1], f3.at[k, j - 1], (2 * peer + x, c))
+
+    def pair_y(k):
+        value = b2[k, z].astype(F32)
+        for j in range(1, half):
+            arrived(a3.at[k, j - 1], f3.at[k, j - 1])
+            value = value + a3[k, j - 1].astype(F32)
+        a4[k, y] = value.astype(BF16)
+        for j in range(1, duo):
+            target = (d, 2 * lax.rem(y + j, duo) + core)
+            push(a4.at[k, y], a4.at[k, y], e4.at[k, j - 1], f4.at[k, j - 1], target)
+
+    def pair_done(k):
+        for j in range(1, duo):
+            arrived(a4.at[k, lax.rem(y - j + duo, duo)], f4.at[k, j - 1])
+        value = a4[k, 0].astype(F32)
+        for j in range(1, duo):
+            value = value + a4[k, j].astype(F32)
+        piece = fin.at[2 * (chunks * duo + k) + core]
+        piece[...] = value.astype(BF16)
+        push(piece, piece, e5.at[k], f5.at[k], other)
+
     stages = (stage_core, stage_y, stage_x, stage_z, stage_cand)
-    places = batches + 1
-    plan = stage_slots(duos, chunks, m, places)
+    pair_stages = (pair_core, pair_x, pair_z, pair_y, pair_done)
+    singles = a1.shape[0]
+    blocks = 2 if pairs % 2 == 0 else 1
+    size = pairs // blocks
+    places = blocks + 2
+    plan = []
+    for k in range(chunks):
+        for stage, slot in enumerate((0, 2 + k, 12 + 7 * k, 18 + 7 * k, 27 + 7 * k)):
+            plan.append((slot, stage, stages[stage], k))
+    for k in range(singles):
+        hp = chunks * duo + k - duos
+        ready = places * hp + places - 1 if hp >= 0 else 0
+        for stage, slot in enumerate((0, 2, 9, 18, 22)):
+            plan.append((ready + slot, 5 + stage, pair_stages[stage], k))
+    plan.sort(key=lambda item: (item[0], item[1] % 5, item[3]))
     last = places * duos
 
     def run(hp, place):
-        for step in range(duos):
-            items = [item for item in plan if item[0] == places * step + place]
-            if items:
-                @pl.when(hp == step)
-                def _():
-                    for _, stage, k in items:
-                        stages[stage](k)
+        with jax.named_scope('bw_run'):
+            for step in range(duos):
+                items = [item for item in plan if item[0] == places * step + place]
+                if items:
+                    @pl.when(hp == step)
+                    def _():
+                        for _, _, act, k in items:
+                            act(k)
+
+    def differentiate(hp, i):
+        probs = p_scr[hp, i].astype(F32)
+        dp = dp_scr[hp, i]
+        dlog = []
+        for t in range(2):
+            term = probs[t] * jnp.broadcast_to(dp[t : t + 1], (seq, seq)).T
+            dlog.append((term - probs[t] * jnp.sum(term, axis=0, keepdims=True)).astype(BF16))
+        q2 = stack_halves(qk_scr[hp, i, :, :lanes], low, high)
+        k2 = stack_halves(qk_scr[hp, i, :, lanes:], low, high)
+        dk = jnp.dot(jnp.concatenate(dlog, axis=1), q2, preferred_element_type=F32)
+        dq = lax.dot_general(jnp.concatenate(dlog, axis=0), k2, TN, preferred_element_type=F32)
+        dqk_scr[i, :, :lanes] = dq.astype(BF16)
+        dqk_scr[i, :, lanes:] = dk.astype(BF16)
 
     def backward_step(hp, carry):
-        for b in range(batches):
+        for b in range(blocks):
             run(hp, b)
-            for j in range(batch):
-                i = b * batch + j
-                probs = p_scr[hp, i].astype(F32)
-                term = probs * dp_scr[hp, i][:, None, :]
-                dlog = (term - probs * jnp.sum(term, axis=-1, keepdims=True)).astype(BF16)
-                wide = jnp.concatenate([dlog[0], dlog[1]], axis=1)
-                q2 = stack_halves(qk_scr[hp, i, :, :lanes], low, high)
-                k2 = stack_halves(qk_scr[hp, i, :, lanes:], low, high)
-                dq = jnp.dot(wide, k2, preferred_element_type=F32)
-                dk = lax.dot_general(dlog.reshape(2 * seq, seq), q2, TN, preferred_element_type=F32)
-                dqk_scr[i, :, :lanes] = dq.astype(BF16)
-                dqk_scr[i, :, lanes:] = dk.astype(BF16)
-        grad = jnp.dot(nt_scr[...], dqk_scr[...].reshape(pairs * seq, 2 * lanes), preferred_element_type=F32)
-        grads[duos + hp, 0] = grad[:, :lanes].reshape(half, 2, rows, lanes).astype(BF16)
-        grads[duos + hp, 1] = grad[:, lanes:].reshape(half, 2, rows, lanes).astype(BF16)
-        run(hp, batches)
+
+            @pl.when(hp < duos)
+            def _():
+                with jax.named_scope('bw_block'):
+                    for j in range(size):
+                        differentiate(hp, b * size + j)
+
+        run(hp, blocks)
+
+        @pl.when(hp < duos)
+        def _():
+            with jax.named_scope('bw_dot'):
+                grad = jnp.dot(nt_scr[...], dqk_scr[...].reshape(pairs * seq, 2 * lanes), preferred_element_type=F32)
+                grads[duos + hp, 0] = grad[:, :lanes].reshape(half, 2, rows, lanes).astype(BF16)
+                grads[duos + hp, 1] = grad[:, lanes:].reshape(half, 2, rows, lanes).astype(BF16)
+
+        run(hp, blocks + 1)
         return carry
 
     lax.fori_loop(0, duos, backward_step, 0)
-    for slot, stage, k in plan:
+    for slot, stage, act, k in plan:
         if slot >= last:
-            stages[stage](k)
-    for k in range(chunks):
+            with jax.named_scope('tail_%d_%d' % (stage, k)):
+                act(k)
+    with jax.named_scope('fin_wait'):
+      for k in range(chunks):
         for j in range(1, m):
             arrived(fin.at[k * m + lax.rem(c - j + m, m)], v5.at[k, j - 1])
+      for k in range(singles):
+        arrived(fin.at[2 * (chunks * duo + k) + 1 - core], f5.at[k])
     part = jnp.zeros((8, lanes), F32)
     for g in range(groups):
         block = fin[g].astype(F32).reshape(rows // 8, 8, lanes)
@@ -418,7 +513,8 @@
     r6[d] = part
     for j in range(1, n):
         push(sq, r6.at[d], t6.at[j - 1], v6.at[j - 1], (lax.rem(d + j, n), c))
-    for j in range(1, n):
+    with jax.named_scope('sq_wait'):
+      for j in range(1, n):
         arrived(r6.at[lax.rem(d - j + n, n)], v6.at[j - 1])
     count = groups * lanes * n * rows
     squares = jnp.sum(jnp.sum(jnp.sum(r6[...], axis=0), axis=0, keepdims=True), axis=1, keepdims=True)
@@ -431,8 +527,9 @@
     for r in range(late_rounds):
         arrived(w_scr.at[0, 0 : half - 1, 0], zb_s.at[r])
         arrived(w_scr.at[0, :, 0], xb_s.at[r])
-        for j in range(duo - 1):
-            arrived(w_scr.at[0], yb_s.at[r, j])
+        for place in range(2):
+            for j in range(duo - 1):
+                arrived(w_scr.at[0, :, 0], yb_s.at[r, place, j])
         for j in range(duo):
             arrived(w_scr.at[0], cb_s.at[r, j])
     for j in range(m - 1):
@@ -446,26 +543,16 @@
             arrived(r4.at[k, j], t4.at[k, j])
         for j in range(m - 1):
             arrived(fin.at[k * m + c], t5.at[k, j])
+    for k in range(singles):
+        arrived(a1.at[k], e1.at[k])
+        arrived(a2.at[k], e2.at[k])
+        for j in range(half - 1):
+            arrived(a3.at[k, j], e3.at[k, j])
+        for j in range(duo - 1):
+            arrived(a4.at[k, 0], e4.at[k, j])
+        arrived(fin.at[0], e5.at[k])
     for j in range(n - 1):
         arrived(sq, t6.at[j])
-
-
-def stage_slots(duos, chunks, m, places):
-    plan = []
-    previous = [0] * 5
-    for k in range(chunks):
-        done = (k + 1) * m - 2 * duos
-        first = 0 if done <= 0 else places * (-(-done // 2)) - 1
-        slots = [first]
-        for gap in (2, 6, 4, 4):
-            slots.append(slots[-1] + gap)
-        for stage in range(5):
-            slots[stage] = max(slots[stage], previous[stage] + (0 if stage == 0 else 3))
-            if stage:
-                slots[stage] = max(slots[stage], slots[stage - 1] + 1)
-            plan.append((slots[stage], stage, k))
-        previous = slots
-    return sorted(plan)
 
 
 def finish_kernel(duos, fin, scale_ref, loss_in, out_ref, loss_ref):
@@ -494,7 +581,8 @@
     early_rounds, late_rounds = early // 2, (groups - early) // m
     batch = 4 if pairs % 4 == 0 else 1
     hpad = -(-heads // 16) * 16
-    chunks = groups // m
+    chunks = duos // duo
+    singles = 2 * duos - chunks * duo
     near, far = max(duo - 1, 1), max(half - 1, 1)
     dma = pltpu.SemaphoreType.DMA
     vmem = pltpu.VMEM
@@ -533,13 +621,19 @@
             vmem((chunks, half, rows, lanes), BF16),
             vmem((chunks, half, rows, lanes), BF16),
             vmem((chunks, far, rows, lanes), BF16),
+            vmem((singles, half, 2, rows, lanes), BF16),
+            vmem((singles, half, 2, rows, lanes), BF16),
+            vmem((singles, half, rows, lanes), BF16),
+            vmem((singles, half, rows, lanes), BF16),
+            vmem((singles, far, rows, lanes), BF16),
+            vmem((singles, duo, rows, lanes), BF16),
             vmem((8, lanes), F32),
             vmem((n, 8, lanes), F32),
             dma((pairs // batch,)), dma, dma((early_rounds,)), dma((late_rounds,)),
             dma((early_rounds,)), dma((early_rounds,)), dma((early_rounds,)), dma((early_rounds,)),
             dma((early_rounds,)),
             dma((late_rounds,)), dma((late_rounds,)), dma((late_rounds,)), dma((late_rounds,)),
-            dma((late_rounds, near)), dma((late_rounds, duo)), dma((groups,)),
+            dma((late_rounds, 2, near)), dma((late_rounds, 2, near)), dma((late_rounds, duo)), dma((groups,)),
             dma((m - 1,)), dma((m - 1,)),
             dma((chunks,)), dma((chunks,)),
             dma((chunks, near)), dma((chunks, near)),
@@ -547,6 +641,11 @@
             dma((chunks, far)), dma((chunks, far)),
             dma((chunks, m - 1)), dma((chunks, m - 1)),
             dma((n - 1,)), dma((n - 1,)),
+            dma((singles,)), dma((singles,)),
+            dma((singles,)), dma((singles,)),
+            dma((singles, far)), dma((singles, far)),
+            dma((singles, near)), dma((singles, near)),
+            dma((singles,)), dma((singles,)),
         ],
         compiler_params=pltpu.CompilerParams(
             collective_id=0, has_side_effects=True, vmem_limit_bytes=VMEM_LIMIT

time: 125 us -> 89.3 us (0.71)
  Pallas kernels: 124 us -> 88.3 us
    pallas_call x1, Pallas kernels: 121 us -> 86.1 us  [shards(): pl.pallas_call(functools.partial(fused_kernel, n, m, early), in_specs=[sm...]
where the time goes in v2:
time: 89.3 us; the launch traced here: 89.1 us
  Pallas kernels  88.3 us (99%)
    pallas_call x1, Pallas kernels, shards(): pl.pallas_call(functools.partial(fused_kernel, n, m, early), in_specs=[sm...  86.1 us
    pallas_call x1, Pallas kernels, shards(): pl.pallas_call(functools.partial(finish_kernel, duos), in_specs=[here, he...  2.2 us

profile of v2, /device:TPU:0, one launch (start us, length us, event | category | flops | bytes accessed | tf_op | source)
XLA Modules:
  0.0 89.1 jit_solution(9219158156776243345)
XLA Ops:
  0.6 86.1 %fused_step.1 = (bf16[24,96,128]{2,1,0:T(8,128)(2,1)}, f32[8,128]{1,0:T(8,128)}, f32[8,128]{1,0:T(8,128)}) custom-call(s32[2,8]{1,0:T(2,128)} %len_ref.1, s32[2,8]{1,0:T(2,128)} %lab_ref.1, bf16[16,128,768]{2,1,0:T(8,128)(2,1)} %bitcast.1, bf16[96,3072]{1,0:T(8,128)(2,1)} %w_hbm.1, f32[768]{0:T(1024)} %gain_ref.1, f32[12,128,128]{2,1,0:T(8,128)} %bias_hbm.1, ...), custom_call_target="tpu_custom_call" | custom-call | tf_op jit(solution)/shard_map/fused_step/pallas_call | solution.py:593
  86.8 2.2 %finish.1 = (f32[96,3072]{1,0:T(8,128)}, f32[2]{0:T(128)}) custom-call(bf16[24,96,128]{2,1,0:T(8,128)(2,1)} %get-tuple-element.5.fin, f32[8,128]{1,0:T(8,128)} %get-tuple-element.6.scale_ref, f32[8,128]{1,0:T(8,128)} %get-tuple-element.7.loss_in), custom_call_target="tpu_custom_call" | custom-call | tf_op jit(solution)/shard_map/finish/pallas_call | solution.py:655

commit v3 on v2

v3 whole, which is shorter than its diff:
```python
import functools

import jax
import jax.numpy as jnp
from jax import lax
from jax.experimental import pallas as pl
from jax.experimental.pallas import tpu as pltpu
from jax.sharding import PartitionSpec as P

EPS = 1e-06
F32 = jnp.float32
BF16 = jnp.bfloat16
VMEM_LIMIT = 60 * 1024 * 1024
LEAD = 4
NT = (((1,), (1,)), ((), ()))
TN = (((0,), (0,)), ((), ()))
MESH = pl.DeviceIdType.MESH


def half_masks(lanes):
    lane = lax.broadcasted_iota(jnp.int32, (1, lanes), 1)
    low = (lane < lanes // 2).astype(F32)
    return low.astype(BF16), (1.0 - low).astype(BF16)


def stack_halves(block, low, high):
    return jnp.concatenate([block * low, block * high], axis=0)


def head_mask(hpad, width, head_size):
    lane = lax.broadcasted_iota(jnp.int32, (hpad, width), 1)
    head = lax.broadcasted_iota(jnp.int32, (hpad, width), 0)
    start = head * head_size
    return ((lane >= start) & (lane < start + head_size)).astype(F32)


def arrived(ref, sem):
    pltpu.make_async_copy(ref, ref, sem).wait()


def push(src, dst, send, recv, target):
    pltpu.make_async_remote_copy(
        src_ref=src, dst_ref=dst, send_sem=send, recv_sem=recv, device_id=target, device_id_type=MESH
    ).start()


def lengths_column(ref, pairs, per):
    row = lax.broadcasted_iota(jnp.int32, (pairs, 1), 0)
    column = jnp.zeros((pairs, 1), F32)
    for i in range(pairs):
        column = jnp.where(row == i, ref[i // per, i % per].astype(F32), column)
    return column


def fused_kernel(n, m, early, len_ref, lab_ref, h_hbm, w_hbm, gain_ref, bias_hbm, sw_ref,
                 fin_hbm, loss_ref,
                 fin, h_scr, bias_scr, w_scr, norm_scr, nt_scr, qk_scr, p_scr, wsum_scr, u_scr, hsum_scr, ex_scr,
                 dp_scr, dqk_scr, grads, r1, s1, r2, s2, r3, s3, r4, a1, b1, a2, b2, a3, a4, sq, r6,
                 h_sem, b_sem, wa_sem, wb_sem,
                 za_r, xa_r, zb_r, xb_r, yb_r, ga_r, gb_r, few_s, many_s, ex_s, ex_r,
                 t1, v1, t2, v2, t3, v3, t4, v4, t5, v5, t6, v6,
                 e1, f1, e2, f2, e3, f3, e4, f4, e5, f5):
    pairs, seq, width = h_scr.shape
    queries, per = len_ref.shape
    heads = bias_scr.shape[0]
    groups, half, _, rows, lanes = w_scr.shape
    duos = heads // 2
    duo = m // 2
    head_size = width // heads
    hpad = u_scr.shape[1]
    batch = pairs // h_sem.shape[0]
    batches = pairs // batch
    early_rounds = early // 2
    late_rounds = (groups - early) // m
    d, c = lax.axis_index("dp"), lax.axis_index("cand")
    z, x = d // 2, d % 2
    y, core = c // 2, c % 2
    across = (d + 1 - 2 * x, c)
    other = (d, c + 1 - 2 * core)

    lead = LEAD

    def column(g):
        tail = g // (2 * duos)
        return (1 - tail) * (g // 2 + (g % 2) * duos) + tail * g

    early_slots = (0, duos, groups - 4, groups - 2)

    def early_group(a, which):
        return early_slots[a] + which

    def late_group(r, which):
        if r == 0:
            return 2 + which + 2 * (which // 4)
        return 4 + r * m + which

    order = [("late", 0), ("early", 0), ("late", 1), ("early", 1), ("late", 2), ("early", 2), ("late", 3), ("early", 3)]
    order = [(kind, r) for kind, r in order if kind == "early" or r < late_rounds]

    def load(g, sem):
        at = pl.multiple_of(column(g) * lanes, lanes)
        return pltpu.make_async_copy(w_hbm.at[:, pl.ds(at, lanes)], w_scr.at[g, z, x], sem)

    loads = [load(early_group(a, core), wa_sem.at[a]) for a in range(early_rounds)]
    loads += [load(late_group(r, c), wb_sem.at[r, 0]) for r in range(late_rounds)]
    mirrors = [
        [load(late_group(r, 2 * lax.rem(y - j + duo, duo) + core), wb_sem.at[r, j]) for j in range(1, duo)]
        for r in range(late_rounds)
    ]
    tokens = []
    for b in range(batches):
        part = pl.ds(b * batch, batch)
        tokens.append(pltpu.make_async_copy(h_hbm.at[part], h_scr.at[part], h_sem.at[b]))
    bias_load = pltpu.make_async_copy(bias_hbm, bias_scr, b_sem)
    for copy in loads + tokens + [bias_load] + sum(mirrors, []):
        copy.start()
    peers = [(d, lax.rem(c + j, m)) for j in range(1, m)] + [(lax.rem(d + j, n), c) for j in range(1, n)]
    peers += [(lax.rem(d + j, n), other[1]) for j in range(1, n)]
    barrier = pltpu.get_barrier_semaphore()
    for peer in peers:
        pl.semaphore_signal(barrier, inc=1, device_id=peer, device_id_type=MESH)

    col = lax.broadcasted_iota(jnp.int32, (1, seq), 1)
    row = lax.broadcasted_iota(jnp.int32, (seq, 1), 0)
    key = lax.broadcasted_iota(jnp.int32, (2, seq, seq), 1)
    low, high = half_masks(lanes)
    gain = gain_ref[...].reshape(1, width)
    sw = sw_ref[...].reshape(1, width)

    def length_of(i):
        return len_ref[i // per, i % per]

    def normalise(b):
        tokens[b].wait()
        values = h_scr[b * batch : (b + 1) * batch].reshape(batch * seq, width).astype(F32)
        factor = lax.rsqrt(jnp.mean(values * values, axis=-1, keepdims=True) + EPS)
        normed = (values * factor * gain).astype(BF16)
        norm_scr[b * batch : (b + 1) * batch] = normed.reshape(batch, seq, width)
        nt_scr[:, b * batch * seq : (b + 1) * batch * seq] = normed.T
        for j in range(batch):
            i = b * batch + j
            live = (row < length_of(i)).astype(F32)
            hsum_scr[i : i + 1, :] = jnp.sum(values[j * seq : (j + 1) * seq] * live, axis=0, keepdims=True)

    hops = [1] + [half - 1] * (half > 2) + list(range(2, half - 1))

    def send_z(g, s, r, x_s, x_r):
        block = w_scr.at[g, z, x]
        for j in hops:
            push(block, block, s, r.at[j - 1], (2 * lax.rem(z + j, half) + x, c))
        push(block, block, x_s, x_r, across)

    def relay_x(g, z_sem, s, r, also=None):
        for j in hops:
            block = w_scr.at[g, lax.rem(z - j + half, half), x]
            arrived(block, z_sem.at[j - 1])
            push(block, block, s, r, across)
            if also is not None:
                relay_y(block, also, 0)

    def send_round(i):
        if i >= len(order):
            return
        kind, r = order[i]
        if kind == "early":
            loads[r].wait()
            send_z(early_group(r, core), few_s, za_r.at[r], many_s, xa_r.at[r])
        else:
            loads[early_rounds + r].wait()
            send_z(late_group(r, c), few_s, zb_r.at[r], many_s, xb_r.at[r])

    def early_x(a):
        relay_x(early_group(a, core), za_r.at[a], many_s, xa_r.at[a])
        send_round(order.index(("early", a)) + lead)

    def early_core(a):
        g = early_group(a, core)
        arrived(w_scr.at[g, :, 0], xa_r.at[a])
        push(w_scr.at[g], w_scr.at[g], many_s, ga_r.at[a], other)

    def early_ready(a):
        g = early_group(a, 1 - core)
        arrived(w_scr.at[g], ga_r.at[a])

    def relay_y(blocks, r, place):
        for j in range(1, duo):
            target = (d, 2 * lax.rem(y + j, duo) + core)
            push(blocks, blocks, (few_s, many_s)[place], yb_r.at[r, place, j - 1], target)

    def late_x(r):
        relay_x(late_group(r, c), zb_r.at[r], many_s, xb_r.at[r], r)
        send_round(order.index(("late", r)) + lead)

    def late_y(r):
        g = late_group(r, c)
        arrived(w_scr.at[g, :, 0], xb_r.at[r])
        relay_y(w_scr.at[g, :, 1 - x], r, 1)
        push(w_scr.at[g], w_scr.at[g], many_s, gb_r.at[r], other)

    def late_core(r):
        for j in range(1, duo):
            g = late_group(r, 2 * lax.rem(y - j + duo, duo) + core)
            mirrors[r][j - 1].wait()
            arrived(w_scr.at[g, 0 : half - 1, 0], yb_r.at[r, 0, j - 1])
            arrived(w_scr.at[g, :, 0], yb_r.at[r, 1, j - 1])
            push(w_scr.at[g], w_scr.at[g], many_s, gb_r.at[r], other)

    def late_ready(r):
        arrived(w_scr.at[0:duo], gb_r.at[r])

    def relays(todo):
        for act, r in todo:
            if r < (early_rounds if act in (early_x, early_core, early_ready) else late_rounds):
                with jax.named_scope(act.__name__ + '_%d' % r):
                    act(r)

    with jax.named_scope('norm0'):
        normalise(0)
    with jax.named_scope('barrier'):
        pl.semaphore_wait(barrier, len(peers))
    for i in range(lead):
        send_round(i)
    with jax.named_scope('norm'):
        for b in range(1, batches):
            normalise(b)
    with jax.named_scope('bias'):
        bias_load.wait()
        for h in range(heads):
            bias_scr[h] = bias_scr[h].T
    with jax.named_scope('early'):
        relays([(late_x, 0), (early_x, 0), (late_y, 0), (late_x, 1), (early_core, 0), (early_ready, 0)])

    def weight(g):
        value = w_scr[g]
        if rows % 16 == 0:
            return value.reshape(width, lanes)
        return value.astype(F32).reshape(width, lanes).astype(BF16)

    def project(hp):
        both = jnp.concatenate([weight(2 * hp), weight(2 * hp + 1)], axis=1)
        for b in range(batches):
            block = norm_scr[b * batch : (b + 1) * batch].reshape(batch * seq, width)
            proj = jnp.dot(block, both, preferred_element_type=F32)
            qk_scr[hp, b * batch : (b + 1) * batch] = proj.astype(BF16).reshape(batch, seq, 2 * lanes)

    def attend(hp, i):
        length = length_of(i)
        live = (col < length).astype(F32)
        q2 = qk_scr[hp, i, :, :lanes]
        k2 = qk_scr[hp, i, :, lanes:]
        logits = lax.dot_general(stack_halves(k2, low, high), q2, NT, preferred_element_type=F32)
        logits = logits.reshape(2, seq, seq) + bias_scr[pl.ds(2 * hp, 2)]
        logits = jnp.where(key < length, logits, -1e30)
        expo = jnp.exp(logits - jnp.max(logits, axis=1, keepdims=True))
        inv = live[None] / jnp.sum(expo, axis=1, keepdims=True)
        probs = (expo * inv).astype(BF16)
        probs = jnp.stack([probs[0].T, probs[1].T])
        p_scr[hp, i] = probs
        wsum_scr[hp, i] = jnp.sum(probs.astype(F32), axis=1)

    forward_plan = {
        (0, 1): [(early_x, 1), (late_core, 0), (late_y, 1), (late_x, 2)],
        (1, 0): [(late_ready, 0)],
        (1, 1): [(early_core, 1), (early_x, 2)],
        (2, 1): [(late_y, 2), (late_core, 1), (late_x, 3)],
        (3, 0): [(early_ready, 1)],
        (3, 1): [(early_core, 2), (early_x, 3)],
        (4, 0): [(late_ready, 1), (late_y, 3)],
        (4, 1): [(late_core, 2)],
        (5, 0): [(early_core, 3)],
    }

    def forward_step(hp, carry):
        for place in range(2):
            with jax.named_scope('fw_relay'):
                for step in range(duos):
                    todo = forward_plan.get((step, place))
                    if todo:
                        @pl.when(hp == step)
                        def _():
                            relays(todo)

            @pl.when(hp < duos)
            def _():
                with jax.named_scope('fw_block'):
                    if place == 0:
                        project(hp)
                    else:
                        for i in range(pairs):
                            attend(hp, i)

        return carry

    lax.fori_loop(0, duos, forward_step, 0)
    with jax.named_scope('late_core'):
        relays([(late_core, 3)])
    with jax.named_scope('u'):
      for i in range(pairs):
        parts = [wsum_scr[j, i] for j in range(duos)]
        if hpad > heads:
            parts.append(jnp.zeros((hpad - heads, seq), F32))
        weights = jnp.concatenate(parts, axis=0).astype(BF16)
        u_scr[i] = jnp.dot(weights, norm_scr[i], preferred_element_type=F32).astype(BF16)
    with jax.named_scope('late_ready'):
      relays([(late_ready, 2), (late_ready, 3), (early_ready, 2), (early_ready, 3)])

    w_v = jnp.concatenate([weight(2 * duos + j) for j in range(duos)], axis=1)
    w_o = jnp.concatenate([weight(3 * duos + j) for j in range(duos)], axis=1)
    u = u_scr[...].reshape(pairs * hpad, width)
    mixed = jnp.dot(u, w_v, preferred_element_type=F32)
    mask = head_mask(hpad, width, head_size)
    ctx32 = jnp.sum(mixed.reshape(pairs, hpad, width) * mask[None], axis=1)
    ctx = ctx32.astype(BF16)
    share = 1.0 / lengths_column(len_ref, pairs, per)
    mean = ctx32 * share
    mean_high = mean.astype(BF16)
    mean_low = (mean - mean_high.astype(F32)).astype(BF16)
    both = jnp.dot(jnp.concatenate([mean_high, mean_low], axis=0), w_o, preferred_element_type=F32)
    pooled = hsum_scr[...] * share + both[:pairs] + both[pairs:]
    factor = lax.rsqrt(jnp.mean(pooled * pooled, axis=-1, keepdims=True) + EPS)
    score = jnp.sum(pooled * factor * sw, axis=-1, keepdims=True)
    label = lengths_column(lab_ref, pairs, per)
    score = jnp.broadcast_to(score, (pairs, lanes))
    label = jnp.broadcast_to(label, (pairs, lanes))
    ex_scr[c] = jnp.concatenate([score, label], axis=0)
    for j in range(1, m):
        push(ex_scr.at[c], ex_scr.at[c], ex_s, ex_r, (d, lax.rem(c + j, m)))

    dot = jnp.sum(pooled * sw, axis=-1, keepdims=True) * (1.0 / width)
    slope = (factor * sw - pooled * (factor * factor * factor * dot)) * share
    cg = lax.dot_general(slope.astype(BF16), w_o, NT, preferred_element_type=F32)
    spread = (cg[:, None, :] * mask[None]).astype(BF16).reshape(pairs * hpad, width)
    wc = lax.dot_general(spread, w_v, NT, preferred_element_type=F32)
    u_scr_wc = wc.astype(BF16).reshape(pairs, hpad, width)
    for i in range(pairs):
        part = jnp.dot(u_scr_wc[i], nt_scr[:, i * seq : (i + 1) * seq], preferred_element_type=F32)
        for j in range(duos):
            dp_scr[j, i] = part[2 * j : 2 * j + 2]

    with jax.named_scope('ex_wait'):
      arrived(ex_scr.at[0 : m - 1], ex_r)
    all_scores, all_labels = ex_scr[:, :pairs], ex_scr[:, pairs:]
    target = jnp.exp(all_labels)
    own_target = jnp.exp(label)
    query = lax.broadcasted_iota(jnp.int32, (pairs, lanes), 0) // per
    loss_row = lax.broadcasted_iota(jnp.int32, loss_ref.shape, 0)
    loss = jnp.zeros(loss_ref.shape, F32)
    score_grad = jnp.zeros((pairs, lanes), F32)

    def total(values):
        return jnp.sum(jnp.sum(values, axis=0), axis=0, keepdims=True)

    for q in range(queries):
        inside = (query == q)[None]
        highest = jnp.max(jnp.max(jnp.where(inside, all_scores, -3e38), axis=0), axis=0, keepdims=True)
        expsum = total(jnp.where(inside, jnp.exp(all_scores - highest[None]), 0.0))
        target_sum = total(jnp.where(inside, target, 0.0))
        target_dot = total(jnp.where(inside, target * all_scores, 0.0))
        loss = jnp.where(loss_row == q + 1, highest + jnp.log(expsum) - target_dot / target_sum, loss)
        own = jnp.exp(score - highest) / expsum - own_target / target_sum
        score_grad = jnp.where(query == q, own, score_grad)
    loss_ref[...] = loss
    sg = score_grad[:, :1]
    out_grad = (slope * sg).astype(BF16)
    spread = (cg * sg).astype(BF16).astype(F32)
    spread = (spread[:, None, :] * mask[None]).astype(BF16).reshape(pairs * hpad, width)
    gv = lax.dot_general(u, spread, TN, preferred_element_type=F32).astype(BF16)
    go = lax.dot_general(ctx, out_grad, TN, preferred_element_type=F32).astype(BF16)
    for t in range(2 * duos):
        source = (gv, go)[t // duos]
        at = (t % duos) * lanes
        grads[t // 2, t % 2] = source[:, at : at + lanes].reshape(half, 2, rows, lanes)
    for i in range(pairs):
        for j in range(duos):
            dp_scr[j, i] = dp_scr[j, i] * sg[i : i + 1]

    chunks = r1.shape[0]

    def finish_chunks(part, waiting, square):
        with jax.named_scope('chunk_wait'):
            if waiting:
                arrived(fin.at[0 : len(waiting) * (m - 1)], v5)
            for g in range(len(waiting) * m):
                part = part + square(g)
        return part

    def stage_core(k):
        push(grads.at[k * duo : (k + 1) * duo, 1 - core], r1.at[k], t1, v1.at[k], other)

    def stage_y(k):
        arrived(r1.at[k], v1.at[k])
        s1[k] = (grads[k * duo : (k + 1) * duo, core].astype(F32) + r1[k].astype(F32)).astype(BF16)
        for j in range(1, duo):
            peer = lax.rem(y + j, duo)
            push(s1.at[k, peer], r2.at[k, j - 1], t2, v2.at[k], (d, 2 * peer + core))

    def stage_x(k):
        value = s1[k, y].astype(F32)
        if duo > 1:
            arrived(r2.at[k], v2.at[k])
        for j in range(1, duo):
            value = value + r2[k, j - 1].astype(F32)
        s2[k] = value.astype(BF16)
        push(s2.at[k, :, 1 - x], r3.at[k], t3, v3.at[k], across)

    def stage_z(k):
        arrived(r3.at[k], v3.at[k])
        s3[k] = (s2[k, :, x].astype(F32) + r3[k].astype(F32)).astype(BF16)
        for j in range(1, half):
            peer = lax.rem(z + j, half)
            push(s3.at[k, peer], r4.at[k, j - 1], t4, v4.at[k], (2 * peer + x, c))

    def stage_cand(k):
        value = s3[k, z].astype(F32)
        if half > 1:
            arrived(r4.at[k], v4.at[k])
        for j in range(1, half):
            value = value + r4[k, j - 1].astype(F32)
        fin[k * m + c] = value.astype(BF16)
        for j in range(1, m):
            piece = fin.at[k * m + c]
            push(piece, piece, t5, v5, (d, lax.rem(c + j, m)))

    def pair_core(k):
        push(grads.at[chunks * duo + k, 1 - core], a1.at[k], e1, f1.at[k], other)

    def pair_x(k):
        arrived(a1.at[k], f1.at[k])
        b1[k] = (grads[chunks * duo + k, core].astype(F32) + a1[k].astype(F32)).astype(BF16)
        push(b1.at[k, :, 1 - x], a2.at[k], e2, f2.at[k], across)

    def pair_z(k):
        arrived(a2.at[k], f2.at[k])
        b2[k] = (b1[k, :, x].astype(F32) + a2[k].astype(F32)).astype(BF16)
        for j in range(1, half):
            peer = lax.rem(z + j, half)
            push(b2.at[k, peer], a3.at[k, j - 1], e3, f3.at[k], (2 * peer + x, c))

    def pair_y(k):
        value = b2[k, z].astype(F32)
        if half > 1:
            arrived(a3.at[k], f3.at[k])
        for j in range(1, half):
            value = value + a3[k, j - 1].astype(F32)
        a4[k, y] = value.astype(BF16)
        for j in range(1, duo):
            target = (d, 2 * lax.rem(y + j, duo) + core)
            push(a4.at[k, y], a4.at[k, y], e4, f4.at[k], target)

    def pair_done(k):
        if duo > 1:
            arrived(a4.at[k, 0 : duo - 1], f4.at[k])
        value = a4[k, 0].astype(F32)
        for j in range(1, duo):
            value = value + a4[k, j].astype(F32)
        piece = fin.at[2 * (chunks * duo + k) + core]
        piece[...] = value.astype(BF16)
        push(piece, piece, e5, f5, other)

    stages = (stage_core, stage_y, stage_x, stage_z, stage_cand)
    pair_stages = (pair_core, pair_x, pair_z, pair_y, pair_done)
    singles = a1.shape[0]
    step_time = 2.25
    plan = []
    for k in range(chunks):
        for stage, at in enumerate((0.0, 1.3 + 0.5 * k, 7.7 + 4.2 * k, 12.4 + 4.2 * k, 18.0 + 4.2 * k)):
            plan.append((at, stage, stages[stage], k))
    for k in range(singles):
        hp = chunks * duo + k - duos
        ready = step_time * (hp + 1) - 0.05 if hp >= 0 else 0.0
        for stage, at in enumerate((0.0, 1.2, 5.6, 11.0, 14.0)):
            plan.append((ready + at, 5 + stage, pair_stages[stage], k))
    plan.sort(key=lambda item: (item[0], item[1] % 5, item[3]))
    slots = [(step_time * hp + at, hp, place) for hp in range(duos)
             for place, at in enumerate((0.0, 1.3, step_time - 0.05))]
    homes = {}
    for item in plan:
        home = next(((hp, place) for at, hp, place in slots if at >= item[0] - 0.1), None)
        homes.setdefault(home, []).append(item)

    def run(hp, place):
        with jax.named_scope('bw_run'):
            for step in range(duos):
                items = homes.get((step, place))
                if items:
                    @pl.when(hp == step)
                    def _():
                        for _, stage, act, k in items:
                            with jax.named_scope('in_%d_%d' % (stage, k)):
                                act(k)

    def differentiate(hp, i):
        probs = p_scr[hp, i].astype(F32)
        term = probs * dp_scr[hp, i][:, None, :]
        dlog = (term - probs * jnp.sum(term, axis=-1, keepdims=True)).astype(BF16)
        wide = jnp.concatenate([dlog[0], dlog[1]], axis=1)
        q2 = stack_halves(qk_scr[hp, i, :, :lanes], low, high)
        k2 = stack_halves(qk_scr[hp, i, :, lanes:], low, high)
        dq = jnp.dot(wide, k2, preferred_element_type=F32)
        dk = lax.dot_general(dlog.reshape(2 * seq, seq), q2, TN, preferred_element_type=F32)
        dqk_scr[i, :, :lanes] = dq.astype(BF16)
        dqk_scr[i, :, lanes:] = dk.astype(BF16)

    def backward_step(hp, carry):
        run(hp, 0)

        @pl.when(hp < duos)
        def _():
            with jax.named_scope('bw_block'):
                for i in range(pairs):
                    differentiate(hp, i)

        run(hp, 1)

        @pl.when(hp < duos)
        def _():
            with jax.named_scope('bw_dot'):
                grad = jnp.dot(nt_scr[...], dqk_scr[...].reshape(pairs * seq, 2 * lanes), preferred_element_type=F32)
                grads[duos + hp, 0] = grad[:, :lanes].reshape(half, 2, rows, lanes).astype(BF16)
                grads[duos + hp, 1] = grad[:, lanes:].reshape(half, 2, rows, lanes).astype(BF16)

        run(hp, 2)
        return carry

    lax.fori_loop(0, duos, backward_step, 0)
    def square(g):
        block = fin[g].astype(F32).reshape(rows // 8, 8, lanes)
        return jnp.sum(block * block, axis=0)

    part = jnp.zeros((8, lanes), F32)
    waiting = [k for k in range(chunks)]
    for _, stage, act, k in homes.get(None, []):
        if stage == 9 and waiting and k == singles - 1:
            part = finish_chunks(part, waiting, square)
            waiting = []
        with jax.named_scope('tail_%d_%d' % (stage, k)):
            act(k)
    if waiting:
        part = finish_chunks(part, waiting, square)
    part = jnp.where(core == 0, part, 0.0)
    for k in range(singles):
        part = part + square(2 * (chunks * duo + k) + core)
    sq[...] = part
    mine = core * n + d
    r6[mine] = part
    targets = [(lax.rem(d + j, n), core) for j in range(1, n)] + [(lax.rem(d + j, n), 1 - core) for j in range(n)]
    for t, (to, to_core) in enumerate(targets):
        push(sq, r6.at[mine], t6, v6, (to, c - core + to_core))
    with jax.named_scope('fin_wait'):
        arrived(fin.at[0:singles], f5)
    store = pltpu.make_async_copy(fin, fin_hbm, b_sem)
    store.start()
    with jax.named_scope('drain'):
        kinds = early_rounds + late_rounds * duo
        arrived(w_scr.at[0:kinds, 0 : half - 1, 0], few_s)
        arrived(w_scr.at[0 : 3 * kinds // 2], many_s)
        arrived(ex_scr.at[0 : m - 1], ex_s)
        if chunks:
            arrived(r1, t1)
            arrived(r3, t3)
            arrived(fin.at[0 : chunks * (m - 1)], t5)
            if duo > 1:
                arrived(r2, t2)
            if half > 1:
                arrived(r4, t4)
        arrived(a1, e1)
        arrived(a2, e2)
        arrived(fin.at[0:singles], e5)
        if half > 1:
            arrived(a3, e3)
        if duo > 1:
            arrived(a4.at[:, 0 : duo - 1], e4)
    with jax.named_scope('sq_wait'):
        arrived(r6.at[0 : 2 * n - 1], v6)
        arrived(r6.at[0 : 2 * n - 1], t6)
    count = groups * lanes * n * rows
    squares = jnp.sum(r6[...], axis=0)
    squares = jnp.sum(jnp.sum(squares, axis=0, keepdims=True), axis=1, keepdims=True)
    loss_ref[0:1, :] = jnp.broadcast_to(1.0 / (jnp.sqrt(squares / count) + EPS), (1, lanes))
    store.wait()


def finish_kernel(duos, fin, loss_in, out_ref, loss_ref):
    groups, rows, lanes = fin.shape
    scale = loss_in[0:1, :]
    for at in range(groups):
        if at < 2 * duos:
            col = 2 * duos + at
        else:
            col = (at % 2) * duos + (at - 2 * duos) // 2
        out_ref[:, col * lanes : (col + 1) * lanes] = fin[at].astype(F32) * scale
    for q in range(loss_ref.shape[0]):
        loss_ref[q] = jnp.max(loss_in[q + 1 : q + 2, :])


def shards(hidden, attn_weight, norm_gain, pos_bias, score_weight, pair_lengths, labels):
    queries, per, seq, width = hidden.shape
    pairs = queries * per
    heads = pos_bias.shape[0]
    n, m = lax.axis_size("dp"), lax.axis_size("cand")
    lanes = 2 * (width // heads)
    duos = heads // 2
    groups = 4 * duos
    rows, half, duo = width // n, n // 2, m // 2
    early = groups // 3
    early_rounds, late_rounds = early // 2, (groups - early) // m
    batch = 4 if pairs % 4 == 0 else 1
    hpad = -(-heads // 16) * 16
    chunks = max(duos // duo - 1, 1)
    singles = 2 * duos - chunks * duo
    near, far = max(duo - 1, 1), max(half - 1, 1)
    dma = pltpu.SemaphoreType.DMA
    vmem = pltpu.VMEM
    here = pl.BlockSpec(memory_space=pltpu.VMEM)
    away = pl.BlockSpec(memory_space=pl.ANY)
    small = pl.BlockSpec(memory_space=pltpu.SMEM)
    loss_rows = -(-(queries + 1) // 8) * 8
    fin, loss = pl.pallas_call(
        functools.partial(fused_kernel, n, m, early),
        in_specs=[small, small, away, away, here, away, here],
        out_specs=[away, here],
        out_shape=[
            jax.ShapeDtypeStruct((groups, rows, lanes), BF16),
            jax.ShapeDtypeStruct((loss_rows, lanes), F32),
        ],
        scratch_shapes=[
            vmem((groups, rows, lanes), BF16),
            vmem((pairs, seq, width), BF16),
            vmem(pos_bias.shape, F32),
            vmem((groups, half, 2, rows, lanes), BF16),
            vmem((pairs, seq, width), BF16),
            vmem((width, pairs * seq), BF16),
            vmem((duos, pairs, seq, 2 * lanes), BF16),
            vmem((duos, pairs, 2, seq, seq), BF16),
            vmem((duos, pairs, 2, seq), F32),
            vmem((pairs, hpad, width), BF16),
            vmem((pairs, width), F32),
            vmem((m, 2 * pairs, lanes), F32),
            vmem((duos, pairs, 2, seq), F32),
            vmem((pairs, seq, 2 * lanes), BF16),
            vmem((2 * duos, 2, half, 2, rows, lanes), BF16),
            vmem((chunks, duo, half, 2, rows, lanes), BF16),
            vmem((chunks, duo, half, 2, rows, lanes), BF16),
            vmem((chunks, near, half, 2, rows, lanes), BF16),
            vmem((chunks, half, 2, rows, lanes), BF16),
            vmem((chunks, half, rows, lanes), BF16),
            vmem((chunks, half, rows, lanes), BF16),
            vmem((chunks, far, rows, lanes), BF16),
            vmem((singles, half, 2, rows, lanes), BF16),
            vmem((singles, half, 2, rows, lanes), BF16),
            vmem((singles, half, rows, lanes), BF16),
            vmem((singles, half, rows, lanes), BF16),
            vmem((singles, far, rows, lanes), BF16),
            vmem((singles, duo, rows, lanes), BF16),
            vmem((8, lanes), F32),
            vmem((2 * n, 8, lanes), F32),
            dma((pairs // batch,)), dma, dma((early_rounds,)), dma((late_rounds, duo)),
            dma((early_rounds, far)), dma((early_rounds,)), dma((late_rounds, far)), dma((late_rounds,)),
            dma((late_rounds, 2, near)), dma((early_rounds,)), dma((late_rounds,)), dma, dma, dma, dma,
            dma, dma((chunks,)), dma, dma((chunks,)), dma, dma((chunks,)), dma, dma((chunks,)), dma, dma, dma, dma,
            dma, dma((singles,)), dma, dma((singles,)), dma, dma((singles,)), dma, dma((singles,)), dma, dma,
        ],
        compiler_params=pltpu.CompilerParams(
            collective_id=0, has_side_effects=True, vmem_limit_bytes=VMEM_LIMIT
        ),
        name="fused_step",
    )(pair_lengths, labels, hidden.reshape(pairs, seq, width), attn_weight, norm_gain, pos_bias, score_weight)
    update, loss = pl.pallas_call(
        functools.partial(finish_kernel, duos),
        in_specs=[here, here],
        out_specs=[here, small],
        out_shape=[
            jax.ShapeDtypeStruct((rows, 4 * width), F32),
            jax.ShapeDtypeStruct((queries,), F32),
        ],
        name="finish",
    )(fin, loss)
    return (update, loss)


def solution(mesh):
    in_specs = (
        P("dp", "cand", None, None),
        P("dp", None),
        P(),
        P(),
        P(),
        P("dp", "cand"),
        P("dp", "cand"),
    )
    out_specs = (P("dp", None), P("dp"))
    return jax.shard_map(shards, mesh=mesh, in_specs=in_specs, out_specs=out_specs, check_vma=False)
```

time: 89.3 us -> 83.1 us (0.931)
  Pallas kernels: 88.3 us -> 82.1 us
    pallas_call x1, Pallas kernels: 86.1 us -> 79.9 us  [shards(): pl.pallas_call(functools.partial(fused_kernel, n, m, early), in_specs=[sm...]
where the time goes in v3:
time: 83.1 us; the launch traced here: 82.9 us
  Pallas kernels  82.1 us (99%)
    pallas_call x1, Pallas kernels, shards(): pl.pallas_call(functools.partial(fused_kernel, n, m, early), in_specs=[sm...  79.9 us
    pallas_call x1, Pallas kernels, shards(): pl.pallas_call(functools.partial(finish_kernel, duos), in_specs=[here, he...  2.2 us

profile of v3, /device:TPU:0, one launch (start us, length us, event | category | flops | bytes accessed | tf_op | source)
XLA Modules:
  0.0 82.9 jit_solution(11533110523136128106)
XLA Ops:
  0.6 79.9 %fused_step.1 = (bf16[24,96,128]{2,1,0:T(8,128)(2,1)}, f32[8,128]{1,0:T(8,128)}) custom-call(s32[2,8]{1,0:T(2,128)} %len_ref.1, s32[2,8]{1,0:T(2,128)} %lab_ref.1, bf16[16,128,768]{2,1,0:T(8,128)(2,1)} %bitcast.1, bf16[96,3072]{1,0:T(8,128)(2,1)} %w_hbm.1, f32[768]{0:T(1024)} %gain_ref.1, f32[12,128,128]{2,1,0:T(8,128)} %bias_hbm.1, f32[768]{0:T(1024)} %sw_ref.1), custom_call_target="tpu_custom_call" | custom-call | tf_op jit(solution)/shard_map/fused_step/pallas_call | solution.py:618
  80.5 2.2 %finish.1 = (f32[96,3072]{1,0:T(8,128)}, f32[2]{0:T(128)}) custom-call(bf16[24,96,128]{2,1,0:T(8,128)(2,1)} %get-tuple-element.4.fin, f32[8,128]{1,0:T(8,128)} %get-tuple-element.5.loss_in), custom_call_target="tpu_custom_call" | custom-call | tf_op jit(solution)/shard_map/finish/pallas_call | solution.py:668

commit v4 on v3

--- a/solution.py
+++ b/solution.py
@@ -12,6 +12,7 @@
 BF16 = jnp.bfloat16
 VMEM_LIMIT = 60 * 1024 * 1024
 LEAD = 4
+FINISH = 2
 NT = (((1,), (1,)), ((), ()))
 TN = (((0,), (0,)), ((), ()))
 MESH = pl.DeviceIdType.MESH
@@ -52,9 +53,9 @@
     return column
 
 
-def fused_kernel(n, m, early, len_ref, lab_ref, h_hbm, w_hbm, gain_ref, bias_hbm, sw_ref,
+def fused_kernel(n, m, early, len_hbm, lab_hbm, h_hbm, w_hbm, gain_hbm, bias_hbm, sw_hbm,
                  fin_hbm, loss_ref,
-                 fin, h_scr, bias_scr, w_scr, norm_scr, nt_scr, qk_scr, p_scr, wsum_scr, u_scr, hsum_scr, ex_scr,
+                 len_ref, lab_ref, gain_ref, sw_ref, small_sem, fin, h_scr, bias_scr, w_scr, norm_scr, nt_scr, qk_scr, p_scr, wsum_scr, u_scr, hsum_scr, ex_scr,
                  dp_scr, dqk_scr, grads, r1, s1, r2, s2, r3, s3, r4, a1, b1, a2, b2, a3, a4, sq, r6,
                  h_sem, b_sem, wa_sem, wb_sem,
                  za_r, xa_r, zb_r, xb_r, yb_r, ga_r, gb_r, few_s, many_s, ex_s, ex_r,
@@ -84,6 +85,15 @@
         tail = g // (2 * duos)
         return (1 - tail) * (g // 2 + (g % 2) * duos) + tail * g
 
+    peers = [(d, lax.rem(c + j, m)) for j in range(1, m)] + [(lax.rem(d + j, n), c) for j in range(1, n)]
+    peers += [(lax.rem(d + j, n), other[1]) for j in range(1, n)]
+    barrier = pltpu.get_barrier_semaphore()
+    for peer in peers:
+        pl.semaphore_signal(barrier, inc=1, device_id=peer, device_id_type=MESH)
+
+    small = [(len_hbm, len_ref), (gain_hbm, gain_ref), (lab_hbm, lab_ref), (sw_hbm, sw_ref)]
+    small = [pltpu.make_async_copy(src, dst, small_sem.at[t]) for t, (src, dst) in enumerate(small)]
+
     early_slots = (0, duos, groups - 4, groups - 2)
 
     def early_group(a, which):
@@ -112,20 +122,12 @@
         part = pl.ds(b * batch, batch)
         tokens.append(pltpu.make_async_copy(h_hbm.at[part], h_scr.at[part], h_sem.at[b]))
     bias_load = pltpu.make_async_copy(bias_hbm, bias_scr, b_sem)
-    for copy in loads + tokens + [bias_load] + sum(mirrors, []):
+    for copy in loads + small + tokens + [bias_load] + sum(mirrors, []):
         copy.start()
-    peers = [(d, lax.rem(c + j, m)) for j in range(1, m)] + [(lax.rem(d + j, n), c) for j in range(1, n)]
-    peers += [(lax.rem(d + j, n), other[1]) for j in range(1, n)]
-    barrier = pltpu.get_barrier_semaphore()
-    for peer in peers:
-        pl.semaphore_signal(barrier, inc=1, device_id=peer, device_id_type=MESH)
-
     col = lax.broadcasted_iota(jnp.int32, (1, seq), 1)
     row = lax.broadcasted_iota(jnp.int32, (seq, 1), 0)
     key = lax.broadcasted_iota(jnp.int32, (2, seq, seq), 1)
     low, high = half_masks(lanes)
-    gain = gain_ref[...].reshape(1, width)
-    sw = sw_ref[...].reshape(1, width)
 
     def length_of(i):
         return len_ref[i // per, i % per]
@@ -214,14 +216,16 @@
                 with jax.named_scope(act.__name__ + '_%d' % r):
                     act(r)
 
-    with jax.named_scope('norm0'):
-        normalise(0)
     with jax.named_scope('barrier'):
         pl.semaphore_wait(barrier, len(peers))
     for i in range(lead):
         send_round(i)
+    for copy in small:
+        copy.wait()
+    gain = gain_ref[...].reshape(1, width)
+    sw = sw_ref[...].reshape(1, width)
     with jax.named_scope('norm'):
-        for b in range(1, batches):
+        for b in range(batches):
             normalise(b)
     with jax.named_scope('bias'):
         bias_load.wait()
@@ -381,7 +385,7 @@
             if waiting:
                 arrived(fin.at[0 : len(waiting) * (m - 1)], v5)
             for g in range(len(waiting) * m):
-                part = part + square(g)
+                part = part + square(2 * duos + g)
         return part
 
     def stage_core(k):
@@ -416,10 +420,16 @@
             arrived(r4.at[k], v4.at[k])
         for j in range(1, half):
             value = value + r4[k, j - 1].astype(F32)
-        fin[k * m + c] = value.astype(BF16)
+        piece = fin.at[2 * duos + k * m + c]
+        piece[...] = value.astype(BF16)
         for j in range(1, m):
-            piece = fin.at[k * m + c]
             push(piece, piece, t5, v5, (d, lax.rem(c + j, m)))
+
+    def pair_column(k, which):
+        at = chunks * duo + k
+        if at < duos:
+            return 2 * duos + 2 * at + which
+        return at - duos + which * duos
 
     def pair_core(k):
         push(grads.at[chunks * duo + k, 1 - core], a1.at[k], e1, f1.at[k], other)
@@ -453,7 +463,7 @@
         value = a4[k, 0].astype(F32)
         for j in range(1, duo):
             value = value + a4[k, j].astype(F32)
-        piece = fin.at[2 * (chunks * duo + k) + core]
+        piece = fin.at[pair_column(k, core)]
         piece[...] = value.astype(BF16)
         push(piece, piece, e5, f5, other)
 
@@ -539,7 +549,7 @@
         part = finish_chunks(part, waiting, square)
     part = jnp.where(core == 0, part, 0.0)
     for k in range(singles):
-        part = part + square(2 * (chunks * duo + k) + core)
+        part = part + square(pair_column(k, core))
     sq[...] = part
     mine = core * n + d
     r6[mine] = part
@@ -580,15 +590,11 @@
     store.wait()
 
 
-def finish_kernel(duos, fin, loss_in, out_ref, loss_ref):
-    groups, rows, lanes = fin.shape
+def finish_kernel(fin, loss_in, out_ref, loss_ref):
+    columns, _, lanes = fin.shape
     scale = loss_in[0:1, :]
-    for at in range(groups):
-        if at < 2 * duos:
-            col = 2 * duos + at
-        else:
-            col = (at % 2) * duos + (at - 2 * duos) // 2
-        out_ref[:, col * lanes : (col + 1) * lanes] = fin[at].astype(F32) * scale
+    for at in range(columns):
+        out_ref[:, at * lanes : (at + 1) * lanes] = fin[at].astype(F32) * scale
     for q in range(loss_ref.shape[0]):
         loss_ref[q] = jnp.max(loss_in[q + 1 : q + 2, :])
 
@@ -617,13 +623,18 @@
     loss_rows = -(-(queries + 1) // 8) * 8
     fin, loss = pl.pallas_call(
         functools.partial(fused_kernel, n, m, early),
-        in_specs=[small, small, away, away, here, away, here],
+        in_specs=[away] * 7,
         out_specs=[away, here],
         out_shape=[
             jax.ShapeDtypeStruct((groups, rows, lanes), BF16),
             jax.ShapeDtypeStruct((loss_rows, lanes), F32),
         ],
         scratch_shapes=[
+            pltpu.SMEM((queries, per), jnp.int32),
+            pltpu.SMEM((queries, per), jnp.int32),
+            vmem((width,), F32),
+            vmem((width,), F32),
+            dma((4,)),
             vmem((groups, rows, lanes), BF16),
             vmem((pairs, seq, width), BF16),
             vmem(pos_bias.shape, F32),
@@ -666,9 +677,13 @@
         name="fused_step",
     )(pair_lengths, labels, hidden.reshape(pairs, seq, width), attn_weight, norm_gain, pos_bias, score_weight)
     update, loss = pl.pallas_call(
-        functools.partial(finish_kernel, duos),
-        in_specs=[here, here],
-        out_specs=[here, small],
+        finish_kernel,
+        grid=(FINISH,),
+        in_specs=[
+            pl.BlockSpec((groups // FINISH, rows, lanes), lambda i: (i, 0, 0)),
+            pl.BlockSpec(loss.shape, lambda i: (0, 0)),
+        ],
+        out_specs=[pl.BlockSpec((rows, 4 * width // FINISH), lambda i: (0, i)), small],
         out_shape=[
             jax.ShapeDtypeStruct((rows, 4 * width), F32),
             jax.ShapeDtypeStruct((queries,), F32),

time: 83.1 us -> 82.3 us (level)
  no operation moved by 1% of the time
where the time goes in v4:
time: 82.3 us; the launch traced here: 82.1 us
  Pallas kernels  81.5 us (99%)
    pallas_call x1, Pallas kernels, shards(): pl.pallas_call(functools.partial(fused_kernel, n, m, early), in_specs=[aw...  79.5 us
    pallas_call x1, Pallas kernels, shards(): pl.pallas_call(finish_kernel, grid=(FINISH,), in_specs=[pl.BlockSpec((gro...  2.04 us

profile of v4, /device:TPU:0, one launch (start us, length us, event | category | flops | bytes accessed | tf_op | source)
XLA Modules:
  0.0 82.1 jit_solution(1865285394437389440)
XLA Ops:
  0.6 79.5 %fused_step.1 = (bf16[24,96,128]{2,1,0:T(8,128)(2,1)}, f32[8,128]{1,0:T(8,128)}) custom-call(s32[2,8]{1,0:T(2,128)} %len_hbm.1, s32[2,8]{1,0:T(2,128)} %lab_hbm.1, bf16[16,128,768]{2,1,0:T(8,128)(2,1)} %bitcast.1, bf16[96,3072]{1,0:T(8,128)(2,1)} %w_hbm.1, f32[768]{0:T(1024)} %gain_hbm.1, f32[12,128,128]{2,1,0:T(8,128)} %bias_hbm.1, f32[768]{0:T(1024)} %sw_hbm.1), custom_call_target="tpu_custom_call" | custom-call | tf_op jit(solution)/shard_map/fused_step/pallas_call | solution.py:624
  80.1 2.0 %finish.1 = (f32[96,3072]{1,0:T(8,128)}, f32[2]{0:T(128)}) custom-call(bf16[24,96,128]{2,1,0:T(8,128)(2,1)} %get-tuple-element.4.fin, f32[8,128]{1,0:T(8,128)} %get-tuple-element.5.loss_in), custom_call_target="tpu_custom_call" | custom-call | tf_op jit(solution)/shard_map/finish/pallas_call | solution.py:679

commit v5 on v4

--- a/solution.py
+++ b/solution.py
@@ -368,16 +368,6 @@
     out_grad = (slope * sg).astype(BF16)
     spread = (cg * sg).astype(BF16).astype(F32)
     spread = (spread[:, None, :] * mask[None]).astype(BF16).reshape(pairs * hpad, width)
-    gv = lax.dot_general(u, spread, TN, preferred_element_type=F32).astype(BF16)
-    go = lax.dot_general(ctx, out_grad, TN, preferred_element_type=F32).astype(BF16)
-    for t in range(2 * duos):
-        source = (gv, go)[t // duos]
-        at = (t % duos) * lanes
-        grads[t // 2, t % 2] = source[:, at : at + lanes].reshape(half, 2, rows, lanes)
-    for i in range(pairs):
-        for j in range(duos):
-            dp_scr[j, i] = dp_scr[j, i] * sg[i : i + 1]
-
     chunks = r1.shape[0]
 
     def finish_chunks(part, waiting, square):
@@ -474,12 +464,14 @@
     plan = []
     for k in range(chunks):
         for stage, at in enumerate((0.0, 1.3 + 0.5 * k, 7.7 + 4.2 * k, 12.4 + 4.2 * k, 18.0 + 4.2 * k)):
-            plan.append((at, stage, stages[stage], k))
+            if stage:
+                plan.append((at, stage, stages[stage], k))
     for k in range(singles):
         hp = chunks * duo + k - duos
         ready = step_time * (hp + 1) - 0.05 if hp >= 0 else 0.0
         for stage, at in enumerate((0.0, 1.2, 5.6, 11.0, 14.0)):
-            plan.append((ready + at, 5 + stage, pair_stages[stage], k))
+            if hp >= 0 or stage:
+                plan.append((ready + at, 5 + stage, pair_stages[stage], k))
     plan.sort(key=lambda item: (item[0], item[1] % 5, item[3]))
     slots = [(step_time * hp + at, hp, place) for hp in range(duos)
              for place, at in enumerate((0.0, 1.3, step_time - 0.05))]
@@ -487,6 +479,21 @@
     for item in plan:
         home = next(((hp, place) for at, hp, place in slots if at >= item[0] - 0.1), None)
         homes.setdefault(home, []).append(item)
+
+    def keep(source, base):
+        for t in range(duos):
+            at = (base + t) // 2, (base + t) % 2
+            grads[at] = source[:, t * lanes : (t + 1) * lanes].reshape(half, 2, rows, lanes)
+
+    keep(lax.dot_general(ctx, out_grad, TN, preferred_element_type=F32).astype(BF16), duos)
+    for k in range(duos - chunks * duo):
+        pair_core(k)
+    keep(lax.dot_general(u, spread, TN, preferred_element_type=F32).astype(BF16), 0)
+    for k in range(chunks):
+        stage_core(k)
+    for i in range(pairs):
+        for j in range(duos):
+            dp_scr[j, i] = dp_scr[j, i] * sg[i : i + 1]
 
     def run(hp, place):
         with jax.named_scope('bw_run'):

time: 82.3 us -> 82.3 us (level)
  no operation moved by 1% of the time
where the time goes in v5:
time: 82.3 us; the launch traced here: 82.1 us
  Pallas kernels  81.5 us (99%)
    pallas_call x1, Pallas kernels, shards(): pl.pallas_call(functools.partial(fused_kernel, n, m, early), in_specs=[aw...  79.4 us
    pallas_call x1, Pallas kernels, shards(): pl.pallas_call(finish_kernel, grid=(FINISH,), in_specs=[pl.BlockSpec((gro...  2.04 us

profile of v5, /device:TPU:0, one launch (start us, length us, event | category | flops | bytes accessed | tf_op | source)
XLA Modules:
  0.0 82.1 jit_solution(4824028666795579082)
XLA Ops:
  0.6 79.4 %fused_step.1 = (bf16[24,96,128]{2,1,0:T(8,128)(2,1)}, f32[8,128]{1,0:T(8,128)}) custom-call(s32[2,8]{1,0:T(2,128)} %len_hbm.1, s32[2,8]{1,0:T(2,128)} %lab_hbm.1, bf16[16,128,768]{2,1,0:T(8,128)(2,1)} %bitcast.1, bf16[96,3072]{1,0:T(8,128)(2,1)} %w_hbm.1, f32[768]{0:T(1024)} %gain_hbm.1, f32[12,128,128]{2,1,0:T(8,128)} %bias_hbm.1, f32[768]{0:T(1024)} %sw_hbm.1), custom_call_target="tpu_custom_call" | custom-call | tf_op jit(solution)/shard_map/fused_step/pallas_call | solution.py:631
  80.1 2.0 %finish.1 = (f32[96,3072]{1,0:T(8,128)}, f32[2]{0:T(128)}) custom-call(bf16[24,96,128]{2,1,0:T(8,128)(2,1)} %get-tuple-element.4.fin, f32[8,128]{1,0:T(8,128)} %get-tuple-element.5.loss_in), custom_call_target="tpu_custom_call" | custom-call | tf_op jit(solution)/shard_map/finish/pallas_call | solution.py:686
